TPU v7x, 128 devices: a whole 4x4x4 slice. The times are simulated.
128 devices in a mesh: psg: 16 (over x_hi, y, core), qry: 8 (over z, x_lo).
Axes of the slice: x: 4 (x_hi: 2, x_lo: 2; x = x_hi * 2 + x_lo), y: 4, z: 4, core: 2. Of those that a mesh axis runs over, the one named last changes fastest.
Arguments:
- hidden: bfloat16 [1024, 4096], P('qry'), may hold values from -6 to 6
- norm_gain: float32 [4096], replicated, may hold values from 0.5 to 1.5
- proj_weight: bfloat16 [4096, 4096], P('psg', 'qry'), may hold values from -0.09375 to 0.09375
- pq_codes: int32 [32768, 512], P('psg', 'qry'), may hold values from 0 to 255
- codebook: bfloat16 [512, 8, 256], P('qry'), may hold values from -560 to 560
- positives: int32 [1024], replicated, may hold values from 0 to 32767
Outputs:
- losses: float32 [1024], P('qry')
- hidden_grad: bfloat16 [1024, 4096], P('qry')
- weight_grad: float32 [4096, 4096], P('psg', 'qry')
- codebook_grad: float32 [512, 8, 256], P('qry')
All inputs are finite; a program needn't handle non-finite values.
Results may differ from a plain program's by a relative error of at most 0.019.
The roundings to bfloat16 on the way count: a program that leaves them out, or rounds other values in their place, can miss the bound.
Values may be sent and summed in bfloat16 or wider, within the bound.
A program may use at most 128 MiB of HBM per device.

v0:
```python
import jax
import jax.numpy as jnp
from jax import lax
from jax.sharding import Mesh
from jax.sharding import PartitionSpec as P

QRY = ("qry_0", "qry_1")


score_scale = 0.0625
norm_eps = 1e-06


def summed_rows(x, axes, dim):
    if not axes:
        return x
    nearer = lax.psum_scatter(x, axes[0], scatter_dimension=dim, tiled=True)
    return summed_rows(nearer, axes[1:], dim)


def sent_to_all(x, axis):
    copies = jnp.broadcast_to(x, (lax.axis_size(axis), *x.shape))
    return lax.all_to_all(copies, axis, split_axis=0, concat_axis=0, tiled=True)


def gathered_once(x, axis):
    leaves = jax.tree.leaves(x)
    turns = sorted(range(len(leaves)), key=lambda k: -leaves[k].size)
    width = (1, *leaves[turns[0]].shape)[-1]
    lines = [
        jnp.pad(leaves[k].reshape(-1), (0, -leaves[k].size % width)).reshape(-1, width)
        for k in turns
    ]
    both, at, found = (sent_to_all(jnp.concatenate(lines), axis), 0, {})
    for k, line in zip(turns, lines):
        piece = both[:, at : at + len(line)].reshape(len(both), -1)
        found[k] = piece[:, : leaves[k].size].reshape(-1, *leaves[k].shape)
        at += len(line)
    numbers = iter(range(len(leaves)))
    return jax.tree.map(lambda _: found[next(numbers)], x)


def folded_in_pairs(pieces, combine):
    while len(jax.tree.leaves(pieces)[0]) > 1:
        pieces = jax.vmap(combine)(
            *(jax.tree.map(lambda part: part[side::2], pieces) for side in (0, 1))
        )
    return jax.tree.map(lambda part: part[0], pieces)


def joined_all(x, axis, combine):
    pieces = gathered_once(x, axis)
    return folded_in_pairs(pieces, combine)


def code_hot(code_block, book):
    levels = lax.broadcasted_iota(jnp.int32, code_block.shape + (book.shape[2],), 2)
    return (code_block[:, :, None] == levels).astype(jnp.bfloat16)


def per_device(hidden, norm_gain, proj_weight, pq_codes, codebook, positives):
    gathered = lax.all_gather(hidden, QRY, axis=0, tiled=True)
    floats_all = gathered.astype(jnp.float32)
    inverse_all = lax.rsqrt(jnp.mean(floats_all * floats_all, axis=1, keepdims=True) + norm_eps)
    normed = (floats_all * inverse_all * norm_gain[None, :]).astype(jnp.bfloat16)
    columns = proj_weight.shape[1]
    whole_weight = lax.all_gather(proj_weight, "psg", axis=0, tiled=True)
    query_float = jnp.dot(normed, whole_weight, preferred_element_type=jnp.float32)
    queries = query_float.astype(jnp.bfloat16)
    passage_count = pq_codes.shape[0]
    sub_count = codebook.shape[0]
    sub_width = codebook.shape[1]
    block_rows = min(passage_count, 512)
    code_blocks = pq_codes.reshape(passage_count // block_rows, block_rows, sub_count)

    def decode(code_block):
        hot_table = code_hot(code_block, codebook)
        vectors = jnp.einsum(
            "pmk,mdk->pmd", hot_table, codebook, preferred_element_type=jnp.float32
        )
        return vectors.astype(jnp.bfloat16).reshape(block_rows, columns)

    passages = lax.map(decode, code_blocks).reshape(passage_count, columns)
    partial_value = (
        lax.dot_general(
            queries, passages, (((1,), (1,)), ((), ())), preferred_element_type=jnp.float32
        )
        * score_scale
    )
    qry_index = lax.axis_index(QRY)
    own_rows = hidden.shape[0]
    scores = summed_rows(partial_value, QRY, 0)
    row_targets = lax.dynamic_slice_in_dim(positives, qry_index * own_rows, own_rows, 0)
    local_target = row_targets - lax.axis_index("psg") * passage_count
    target = lax.broadcasted_iota(jnp.int32, scores.shape, 1) == local_target[:, None]
    local_max = jnp.max(scores, axis=1)
    positive_part = jnp.sum(jnp.where(target, scores, 0.0), axis=1)
    local_total = jnp.sum(jnp.exp(scores - local_max[:, None]), axis=1)

    def combine(first, second):
        higher = jnp.maximum(first[0], second[0])
        joined = first[1] * jnp.exp(first[0] - higher) + second[1] * jnp.exp(second[0] - higher)
        return (higher, joined, first[2] + second[2])

    row_max, row_total, positive_score = joined_all(
        (local_max, local_total, positive_part), "psg", combine
    )
    losses = jnp.log(row_total) + row_max - positive_score
    score_grad = (
        jnp.exp(scores - row_max[:, None]) / row_total[:, None] - target.astype(jnp.float32)
    ).astype(jnp.bfloat16)
    all_grad = lax.all_gather(score_grad, QRY, axis=0, tiled=True)
    query_part = jnp.dot(all_grad, passages, preferred_element_type=jnp.float32) * score_scale
    query_grad = lax.psum(query_part, "psg").astype(jnp.bfloat16)
    passage_grad = (
        lax.dot_general(
            all_grad, queries, (((0,), (0,)), ((), ())), preferred_element_type=jnp.float32
        )
        * score_scale
    ).astype(jnp.bfloat16)
    grad_blocks = passage_grad.reshape(
        passage_count // block_rows, block_rows, sub_count, sub_width
    )

    def add_book(carry, paired):
        code_block, grad_block = paired
        hot_table = code_hot(code_block, codebook)
        return (
            carry
            + jnp.einsum("pmk,pmd->mdk", hot_table, grad_block, preferred_element_type=jnp.float32),
            None,
        )

    book_part, unused = lax.scan(
        add_book, jnp.zeros(codebook.shape, jnp.float32), (code_blocks, grad_blocks)
    )
    codebook_grad = lax.psum(book_part.astype(jnp.bfloat16), "psg").astype(jnp.float32)
    row_span = proj_weight.shape[0]
    normed_rows = lax.dynamic_slice_in_dim(normed, lax.axis_index("psg") * row_span, row_span, 1)
    weight_grad = lax.dot_general(
        normed_rows, query_grad, (((0,), (0,)), ((), ())), preferred_element_type=jnp.float32
    )
    norm_part = lax.dot_general(
        query_grad, whole_weight, (((1,), (1,)), ((), ())), preferred_element_type=jnp.float32
    )
    norm_back = lax.psum_scatter(
        norm_part.astype(jnp.bfloat16), QRY, scatter_dimension=0, tiled=True
    ).astype(jnp.float32)
    floats_own = hidden.astype(jnp.float32)
    inverse_own = lax.rsqrt(jnp.mean(floats_own * floats_own, axis=1, keepdims=True) + norm_eps)
    scaled = norm_back * norm_gain[None, :]
    hidden_grad = (
        inverse_own * scaled
        - floats_own
        * inverse_own
        * inverse_own
        * inverse_own
        * jnp.mean(scaled * floats_own, axis=1, keepdims=True)
    ).astype(jnp.bfloat16)
    return (losses, hidden_grad, weight_grad, codebook_grad)


def solution(mesh):
    split = Mesh(mesh.devices.reshape(mesh.shape["psg"], 4, 2), ("psg", "qry_0", "qry_1"))
    return jax.shard_map(
        per_device,
        mesh=split,
        in_specs=(P(QRY, None), P(), P("psg", QRY), P("psg", QRY), P(QRY, None, None), P()),
        out_specs=(P(QRY), P(QRY, None), P("psg", QRY), P(QRY, None, None)),
        check_vma=False,
    )
```

profile of v0, /device:TPU:1, one launch (start us, length us, event | category | flops | bytes accessed | tf_op | source)
XLA Modules:
  0.0 852.5 jit_solution(15345686447529952865)
XLA Ops:
  9.8 33.1 %while.21 = (s32[]{:T(128)}, bf16[4,512,512]{2,1,0:T(8,128)(2,1)}, s32[4,512,64]{1,2,0:T(8,128)S(1)}, bf16[64,8,256]{2,1,0:T(8,128)(2,1)}, s32[]{:T(128)}) while((s32[]{:T(128)}, bf16[4,512,512]{2,1,0:T(8,128)(2,1)}, s32[4,512,64]{1,2,0:T(8,128)S(1)}, bf16[64,8,256]{2,1,0:T(8,128)(2,1)}, s32[]{:T(128)}) %tuple.74), condition=%wide.region_2.3_spmd, body=%wide.region_1.2_spmd.sunk | while | flops 142868480 | bytes 3277377 | solution.py:83
  9.8 7.2 fusion.43
  18.1 7.2 fusion.43
  26.4 7.2 fusion.43
  34.6 7.2 fusion.43
  42.9 138.0 %all-gather.4.cloned.1.call-done = bf16[1024,4096]{1,0:T(8,128)(2,1)} async-done(((bf16[128,4096]{1,0:T(8,128)(2,1)}), bf16[1024,4096]{1,0:T(8,128)(2,1)}) %all-gather.4.cloned.1.call-update) | async-done | bytes 8388624 | tf_op jit(solution)/shard_map/all_gather | solution.py:62
  180.9 5.1 fusion.10
  186.0 10.3 %fusion.12 = bf16[1024,4096]{1,0:T(8,128)(2,1)} fusion(bf16[1024,4096]{1,0:T(8,128)(2,1)} %all-gather.4.cloned.1.call-done, f32[4096]{0:T(1024)S(1)} %copy-done.1, f32[1024]{0:T(1024)S(1)} %add_rsqrt_fusion), kind=kLoop, calls=%fused_computation.19 | loop fusion | flops 16777216 | bytes 16797696 | tf_op jit(solution)/shard_map/convert_element_type | solution.py:65
  196.3 43.5 %all-gather.6.cloned.1.call-done = bf16[4096,512]{1,0:T(8,128)(2,1)} async-done(((bf16[256,512]{1,0:T(8,128)(2,1)}), bf16[4096,512]{1,0:T(8,128)(2,1)}) %all-gather.6.cloned.1.call-update) | async-done | bytes 4194320 | tf_op jit(solution)/shard_map/all_gather | solution.py:67
  239.8 9.1 %convolution_convert_fusion.1 = bf16[1024,512]{1,0:T(8,128)(2,1)S(1)} fusion(bf16[1024,4096]{1,0:T(8,128)(2,1)} %fusion.12, bf16[4096,512]{1,0:T(8,128)(2,1)} %all-gather.6.cloned.1.call-done), kind=kOutput, calls=%fused_computation.35 | convolution fusion | flops 4295491584 | bytes 13631488 | tf_op jit(solution)/shard_map/dot_general | solution.py:68
  249.8 5.6 convolution_multiply_fusion
  255.5 78.3 %reduce-scatter.4.cloned.1.call-done = f32[256,2048]{1,0:T(8,128)} async-done(((f32[1024,2048]{1,0:T(8,128)}), f32[256,2048]{1,0:T(8,128)}) %reduce-scatter.4.cloned.1.call-update) | async-done | bytes 2097168 | tf_op jit(solution)/shard_map/reduce_scatter | solution.py:17
  334.6 35.3 %reduce-scatter.6.cloned.1.call-done = f32[128,2048]{1,0:T(8,128)} async-done(((f32[256,2048]{1,0:T(8,128)}), f32[128,2048]{1,0:T(8,128)}) %reduce-scatter.6.cloned.1.call-update) | async-done | bytes 1048592 | tf_op jit(solution)/shard_map/reduce_scatter | solution.py:17
  372.9 14.4 %all_to_all.5 = f32[16,3,128]{2,1,0:T(4,128)S(1)} all-to-all(f32[16,3,128]{2,1,0:T(4,128)S(1)} %broadcast_in_dim.28), channel_id=1, replica_groups=mesh['psg'=16,'qry_0'=4,'qry_1'=2] {'psg'}, dimensions={0} | all-to-all | bytes 49152 | tf_op jit(solution)/shard_map/all_to_all | solution.py:23
  388.3 2.4 subtract_convert_fusion
  390.8 87.4 %all-gather.8.cloned.1.call-done = bf16[1024,2048]{1,0:T(8,128)(2,1)} async-done(((bf16[128,2048]{1,0:T(8,128)(2,1)}), bf16[1024,2048]{1,0:T(8,128)(2,1)}) %all-gather.8.cloned.1.call-update) | async-done | bytes 4194320 | tf_op jit(solution)/shard_map/all_gather | solution.py:112
  478.2 5.9 multiply_convert_fusion
  484.1 2.9 copy.19
  487.0 2.8 reshape.74
  489.8 3.3 copy.20
  493.1 35.0 %while.22 = (s32[]{:T(128)}, f32[64,8,256]{2,1,0:T(8,128)S(1)}, bf16[4,512,64,8]{1,3,2,0:T(8,128)(2,1)}, s32[4,512,64]{1,2,0:T(8,128)S(1)}, s32[]{:T(128)}, /*index=5*/s32[]{:T(128)}) while((s32[]{:T(128)}, f32[64,8,256]{2,1,0:T(8,128)S(1)}, bf16[4,512,64,8]{1,3,2,0:T(8,128)(2,1)}, s32[4,512,64]{1,2,0:T(8,128)S(1)}, s32[]{:T(128)}, ...), condition=%wide.region_13.14_spmd.clone, body=%wide.region_12.13_spmd.clone.sunk | while | flops 142868480 | bytes 1966675 | solution.py:134
  493.1 8.7 %fusion.45 = f32[64,8,256]{2,1,0:T(8,128)S(1)} fusion(s32[512,64]{0,1:T(8,128)S(1)} %dynamic-slice_bitcast_fusion.5, f32[64,8,256]{2,1,0:T(8,128)S(1)} %get-tuple-element.191, bf16[4,512,64,8]{1,3,2,0:T(8,128)(2,1)} %get-tuple-element.198, s32[]{:T(128)} %get-tuple-element.190, pred[]{:T(512)S(6)} %compare.3), kind=kOutput, calls=%fused_computation.10.clone.1 | convolution fusion | flops 142868480 | bytes 1704449 | tf_op jit(solution)/shard_map/while/body/eval_jaxpr/pmk,pmd->mdk/dot_general | solution.py:130
  501.9 8.7 %fusion.45 = f32[64,8,256]{2,1,0:T(8,128)S(1)} fusion(s32[512,64]{0,1:T(8,128)S(1)} %dynamic-slice_bitcast_fusion.5, f32[64,8,256]{2,1,0:T(8,128)S(1)} %get-tuple-element.191, bf16[4,512,64,8]{1,3,2,0:T(8,128)(2,1)} %get-tuple-element.198, s32[]{:T(128)} %get-tuple-element.190, pred[]{:T(512)S(6)} %compare.3), kind=kOutput, calls=%fused_computation.10.clone.1 | convolution fusion | flops 142868480 | bytes 1704449 | tf_op jit(solution)/shard_map/while/body/eval_jaxpr/pmk,pmd->mdk/dot_general | solution.py:130
  510.6 8.7 %fusion.45 = f32[64,8,256]{2,1,0:T(8,128)S(1)} fusion(s32[512,64]{0,1:T(8,128)S(1)} %dynamic-slice_bitcast_fusion.5, f32[64,8,256]{2,1,0:T(8,128)S(1)} %get-tuple-element.191, bf16[4,512,64,8]{1,3,2,0:T(8,128)(2,1)} %get-tuple-element.198, s32[]{:T(128)} %get-tuple-element.190, pred[]{:T(512)S(6)} %compare.3), kind=kOutput, calls=%fused_computation.10.clone.1 | convolution fusion | flops 142868480 | bytes 1704449 | tf_op jit(solution)/shard_map/while/body/eval_jaxpr/pmk,pmd->mdk/dot_general | solution.py:130
  519.4 8.7 %fusion.45 = f32[64,8,256]{2,1,0:T(8,128)S(1)} fusion(s32[512,64]{0,1:T(8,128)S(1)} %dynamic-slice_bitcast_fusion.5, f32[64,8,256]{2,1,0:T(8,128)S(1)} %get-tuple-element.191, bf16[4,512,64,8]{1,3,2,0:T(8,128)(2,1)} %get-tuple-element.198, s32[]{:T(128)} %get-tuple-element.190, pred[]{:T(512)S(6)} %compare.3), kind=kOutput, calls=%fused_computation.10.clone.1 | convolution fusion | flops 142868480 | bytes 1704449 | tf_op jit(solution)/shard_map/while/body/eval_jaxpr/pmk,pmd->mdk/dot_general | solution.py:130
  528.9 6.5 convolution_multiply_fusion.1
  535.4 77.4 %all-reduce.4 = bf16[1024,512]{1,0:T(8,128)(2,1)S(1)} all-reduce(f32[1024,512]{1,0:T(8,128)} %convolution_multiply_fusion.1), channel_id=1, replica_groups=mesh['psg'=16,'qry_0'=4,'qry_1'=2] {'psg'}, use_global_device_ids=true, to_apply=%region_9.10 | all-reduce | flops 524288 | bytes 3145728 | tf_op jit(solution)/shard_map/psum | solution.py:114
  612.8 8.9 %convolution_convert_fusion = bf16[1024,4096]{1,0:T(8,128)(2,1)} fusion(bf16[4096,512]{1,0:T(8,128)(2,1)} %all-gather.6.cloned.1.call-done, bf16[1024,512]{1,0:T(8,128)(2,1)S(1)} %all-reduce.4), kind=kOutput, calls=%fused_computation.20 | convolution fusion | flops 4299161600 | bytes 13631488 | tf_op jit(solution)/shard_map/dot_general | solution.py:143
  621.8 2.4 fusion.20
  624.2 44.1 %all-reduce.3.cloned.1.call-done = bf16[64,8,256]{2,1,0:T(8,128)(2,1)} async-done(((bf16[64,8,256]{2,1,0:T(8,128)(2,1)}), bf16[64,8,256]{2,1,0:T(8,128)(2,1)}) %all-reduce.3.cloned.1.call-update) | async-done | bytes 262160 | tf_op jit(solution)/shard_map/psum | solution.py:137
  670.0 170.9 %reduce-scatter.8.cloned.1.call-done = bf16[128,4096]{1,0:T(8,128)(2,1)} async-done(((bf16[1024,4096]{1,0:T(8,128)(2,1)}), bf16[128,4096]{1,0:T(8,128)(2,1)}) %reduce-scatter.8.cloned.1.call-update) | async-done | bytes 1048592 | tf_op jit(solution)/shard_map/reduce_scatter | solution.py:146
  842.7 2.9 fusion.18
  (79 shorter events, 17.2 us)
Async XLA Ops:
  7.2 173.7 %all-gather.4.cloned.1.call-start = ((), (), s32[]{:S(2)}) async-start(), calls=%async_computation.4 | async-start | bytes 9437184 | tf_op jit(solution)/shard_map/all_gather | solution.py:62
  7.9 231.9 %all-gather.6.cloned.1.call-start = ((), (), s32[]{:S(2)}) async-start(), calls=%async_computation.5 | async-start | bytes 4456448 | tf_op jit(solution)/shard_map/all_gather | solution.py:67
  8.6 325.1 %reduce-scatter.4.cloned.1.call-start = ((), (), s32[]{:S(2)}) async-start(), calls=%async_computation.6 | async-start | bytes 10485760 | tf_op jit(solution)/shard_map/reduce_scatter | solution.py:17
  42.9 143.1 %copy-start.1 = (f32[4096]{0:T(1024)S(1)}, f32[4096]{0:T(1024)}, u32[]{:S(2)}) copy-start(f32[4096]{0:T(1024)} %param.11) | copy-start | bytes 49156
  196.3 53.5 %copy-start.2 = (bf16[4,512,512]{2,1,0:T(8,128)(2,1)S(1)}, bf16[4,512,512]{2,1,0:T(8,128)(2,1)}, u32[]{:S(2)}) copy-start(bf16[4,512,512]{2,1,0:T(8,128)(2,1)} %get-tuple-element.48) | copy-start | bytes 6291460
  248.9 1.0 copy-start.3
  255.5 222.7 %copy-start.4 = (bf16[1024,512]{1,0:T(8,128)(2,1)S(1)}, bf16[1024,512]{1,0:T(8,128)(2,1)}, u32[]{:S(2)}) copy-start(bf16[1024,512]{1,0:T(8,128)(2,1)} %copy-done.3) | copy-start | bytes 3145732
  255.5 114.4 %reduce-scatter.6.cloned.1.call-start = ((), (), s32[]{:S(2)}) async-start(), calls=%async_computation.7 | async-start | bytes 3145728 | tf_op jit(solution)/shard_map/reduce_scatter | solution.py:17
  333.8 144.4 %all-gather.8.cloned.1.call-start = ((), (), s32[]{:S(2)}) async-start(), calls=%async_computation.8 | async-start | bytes 4718592 | tf_op jit(solution)/shard_map/all_gather | solution.py:112
  390.7 277.5 %all-reduce.3.cloned.1.call-start = ((), (), s32[]{:S(2)}) async-start(), calls=%async_computation.10 | async-start | bytes 524288 | tf_op jit(solution)/shard_map/psum | solution.py:137
  528.9 312.1 %reduce-scatter.8.cloned.1.call-start = ((), (), s32[]{:S(2)}) async-start(), calls=%async_computation.9 | async-start | bytes 9437184 | tf_op jit(solution)/shard_map/reduce_scatter | solution.py:146
  621.8 219.2 %copy-start = (bf16[128,4096]{1,0:T(8,128)(2,1)S(1)}, bf16[128,4096]{1,0:T(8,128)(2,1)}, u32[]{:S(2)}) copy-start(bf16[128,4096]{1,0:T(8,128)(2,1)} %param.10) | copy-start | bytes 3145732
Sparse Core Ops, SparseCore 0:
  9.6 171.2 all-gather.3
  183.4 56.3 all-gather.5
  255.6 78.1 reduce-scatter.3
  336.0 33.8 reduce-scatter.5
  390.9 87.2 all-gather.7
  529.0 139.1 all-reduce.2
  670.6 170.2 reduce-scatter.7
where the time goes:
time: 854 us; the launch traced here: 852 us
  waiting for transfers between devices  599 us (70%)
  matrix products  102 us (12%)
  blocking collectives  91.8 us (11%)
  other arithmetic  29.4 us (3%)
  local copies, waits for them, and re-layouts  15.8 us (2%)
  between operations  14.3 us (2%)
    reduce_scatter x1, waiting for transfers between devices, per_device(): lax.psum_scatter(norm_part.astype(jnp.bfloat16), QRY, scatter_dimension=0...  171 us
    all_gather x1, waiting for transfers between devices, per_device(): gathered = lax.all_gather(hidden, QRY, axis=0, tiled=True)  138 us
    reduce_scatter x2, waiting for transfers between devices, summed_rows(): nearer = lax.psum_scatter(x, axes[0], scatter_dimension=dim, tiled=True)  114 us
    all_gather x1, waiting for transfers between devices, per_device(): all_grad = lax.all_gather(score_grad, QRY, axis=0, tiled=True)  87.4 us
    psum x1, blocking collectives, per_device(): query_grad = lax.psum(query_part, 'psg').astype(jnp.bfloat16)  77.4 us
    psum x1, waiting for transfers between devices, per_device(): lax.psum(book_part.astype(jnp.bfloat16), 'psg').astype(jnp.float32)  44.1 us
    all_gather x1, waiting for transfers between devices, per_device(): whole_weight = lax.all_gather(proj_weight, 'psg', axis=0, tiled=True)  43.5 us
    dot_general x4, matrix products, add_book(): jnp.einsum('pmk,pmd->mdk', hot_table, grad_block, preferred_element_type=...  34.9 us
  transfers between devices with their start and end apart: 7, of which 7 were waited for; matrix products, arithmetic and copies ran while one was open for 8% of the time, Pallas kernels for 0%

commit v1 on v0

v1 whole, which is shorter than its diff:
```python
import jax
import jax.numpy as jnp
from jax import lax
from jax.experimental import pallas as pl
from jax.experimental.pallas import tpu as pltpu
from jax.sharding import Mesh
from jax.sharding import PartitionSpec as P

AXES = ("xh", "y", "k", "z", "xl")
PSG = ("xh", "y", "k")
QRY = ("z", "xl")

score_scale = 0.0625
norm_eps = 1e-06


def decode_kernel(codes_ref, book_ref, out_ref):
    subs, count = codes_ref.shape
    for tile in range(count // 128):
        block = codes_ref[:, tile * 128:(tile + 1) * 128].astype(jnp.float32).astype(jnp.int32)
        found = []
        for m in range(subs):
            code = jnp.broadcast_to(block[m:m + 1, :], (8, 128))
            low = code & 127
            first = jnp.take_along_axis(book_ref[m * 8:m * 8 + 8, 0:128].astype(jnp.float32), low, axis=1, mode="promise_in_bounds")
            second = jnp.take_along_axis(book_ref[m * 8:m * 8 + 8, 128:256].astype(jnp.float32), low, axis=1, mode="promise_in_bounds")
            found.append(jnp.where(code >= 128, second, first))
        for m in range(0, subs, 2):
            out_ref[m * 8:m * 8 + 16, tile * 128:(tile + 1) * 128] = jnp.concatenate(found[m:m + 2], 0).astype(jnp.bfloat16)

def decode(codes, book):
    subs, count = codes.shape
    step = 16
    return pl.pallas_call(
        decode_kernel,
        grid=(subs // step,),
        in_specs=[pl.BlockSpec((step, count), lambda i: (i, 0)), pl.BlockSpec((step * 8, 256), lambda i: (i, 0))],
        out_specs=pl.BlockSpec((step * 8, count), lambda i: (i, 0)),
        out_shape=jax.ShapeDtypeStruct((subs * 8, count), jnp.bfloat16),
        name="decode",
    )(codes, book)

def book_kernel(codes_ref, queries_ref, sg_ref, out_ref, pg_ref, hot_ref, gw_ref):
    count = codes_ref.shape[1]
    pg_ref[...] = (lax.dot_general(queries_ref[...], sg_ref[...], (((0,), (0,)), ((), ())), preferred_element_type=jnp.float32) * 0.0625).astype(jnp.bfloat16)
    levels = lax.broadcasted_iota(jnp.int32, (64, 128), 0)
    for group in range(4):
        for tile in range(count // 128):
            at = slice(tile * 128, (tile + 1) * 128)
            block = codes_ref[group * 8:group * 8 + 8, at].astype(jnp.float32).astype(jnp.int32)
            for m in range(8):
                row = block[m:m + 1, :]
                hi = jnp.broadcast_to(row & 63, (64, 128))
                hot_ref[m * 64:m * 64 + 64, at] = (hi == levels).astype(jnp.float32).astype(jnp.bfloat16)
                lo = jnp.broadcast_to(row >> 6, (8, 128))
                grad = pg_ref[group * 64 + m * 8:group * 64 + m * 8 + 8, at].astype(jnp.float32)
                parts = [jnp.where(lo == t, grad, 0.0) for t in range(4)]
                gw_ref[m * 32:m * 32 + 32, at] = jnp.concatenate(parts, 0).astype(jnp.bfloat16)
        full = lax.dot_general(hot_ref[...], gw_ref[...], (((1,), (1,)), ((), ())), preferred_element_type=jnp.float32)
        own = lax.broadcasted_iota(jnp.int32, (64, 256), 1) // 32
        total = jnp.zeros((64, 256), jnp.float32)
        for m in range(8):
            total = jnp.where(own == m, full[m * 64:m * 64 + 64, :], total)
        out_ref[group] = total

def book_sums(codes, queries, sg):
    subs, count = codes.shape
    rows = queries.shape[0]
    return pl.pallas_call(
        book_kernel,
        grid=(subs // 32,),
        in_specs=[pl.BlockSpec((32, count), lambda i: (i, 0)), pl.BlockSpec((rows, 256), lambda i: (0, i)), pl.BlockSpec((rows, count), lambda i: (0, 0))],
        out_specs=pl.BlockSpec((4, 64, 256), lambda i: (i, 0, 0)),
        out_shape=jax.ShapeDtypeStruct((subs // 8, 64, 256), jnp.float32),
        scratch_shapes=[pltpu.VMEM((256, count), jnp.bfloat16), pltpu.VMEM((512, count), jnp.bfloat16), pltpu.VMEM((256, count), jnp.bfloat16)],
        name="book_sums",
    )(codes, queries, sg)


def unfold(sums):
    groups = sums.shape[0]
    parts = sums.reshape(groups, 64, 8, 4, 8)
    return parts.transpose(0, 2, 4, 3, 1).reshape(groups * 8, 8, 256)


def per_device(hidden, norm_gain, proj_weight, pq_codes, codebook, positives):
    xh, y, k = (lax.axis_index(a) for a in PSG)
    psg = (xh * 4 + y) * 2 + k
    qry = lax.axis_index("z") * 2 + lax.axis_index("xl")
    own_rows, width = hidden.shape
    row_span, columns = proj_weight.shape
    subs = pq_codes.shape[1]
    half = subs // 2
    held = pq_codes.shape[0]
    piece = held // 8

    floats = hidden.astype(jnp.float32)
    inverse = lax.rsqrt(jnp.mean(floats * floats, axis=1, keepdims=True) + norm_eps)
    normed_own = (floats * inverse * norm_gain[None, :]).astype(jnp.bfloat16)
    slice_own = lax.dynamic_slice_in_dim(normed_own, psg * row_span, row_span, 1)
    normed = lax.all_gather(slice_own, QRY, axis=0, tiled=True)

    codes = pq_codes.T.astype(jnp.bfloat16)
    codes = lax.all_to_all(codes, QRY, split_axis=1, concat_axis=0, tiled=True)
    codes = codes.reshape(8, 2, half, piece).transpose(1, 0, 2, 3).reshape(2, 8 * half, piece)
    codes = lax.all_to_all(codes, "k", split_axis=0, concat_axis=2, tiled=True)[0]
    codes = lax.all_gather(codes, "y", axis=1, tiled=True)
    book_half = lax.dynamic_slice_in_dim(codebook, k * half, half, 0).reshape(half * 8, 256)
    book = lax.all_gather(book_half, QRY, axis=0, tiled=True)
    passages = decode(codes, book)

    part = jnp.dot(normed, proj_weight, preferred_element_type=jnp.float32)
    part = lax.psum_scatter(part, "k", scatter_dimension=1, tiled=True)
    part = lax.psum_scatter(part, "y", scatter_dimension=0, tiled=True)
    part = lax.psum_scatter(part, "xh", scatter_dimension=0, tiled=True)
    queries = lax.all_gather(part.astype(jnp.bfloat16), "xh", axis=0, tiled=True)
    queries = lax.all_gather(queries, QRY, axis=1, tiled=True)

    partial_value = jnp.dot(queries, passages, preferred_element_type=jnp.float32)
    scores = lax.psum_scatter(partial_value, "k", scatter_dimension=0, tiled=True) * score_scale

    block = y * 2 + k
    targets = lax.dynamic_slice_in_dim(positives, block * own_rows, own_rows, 0)
    shard = targets // held
    inside = targets - shard * held
    sixth = inside // piece
    here = (shard // 8 == xh) & (sixth == qry)
    column = jnp.where(here, (shard % 8) * piece + inside % piece, -1)
    target = lax.broadcasted_iota(jnp.int32, scores.shape, 1) == column[:, None]
    local_max = jnp.max(scores, axis=1)
    positive_part = jnp.sum(jnp.where(target, scores, 0.0), axis=1)
    local_total = jnp.sum(jnp.exp(scores - local_max[:, None]), axis=1)
    stats = lax.all_gather(
        jnp.stack([local_max, local_total, positive_part]), ("xh", "z", "xl"), axis=0
    )
    row_max = jnp.max(stats[:, 0], axis=0)
    row_total = jnp.sum(stats[:, 1] * jnp.exp(stats[:, 0] - row_max[None, :]), axis=0)
    positive_score = jnp.sum(stats[:, 2], axis=0)
    block_losses = jnp.log(row_total) + row_max - positive_score
    losses = lax.all_gather(block_losses, ("y", "k"), axis=0)
    losses = lax.dynamic_index_in_dim(losses, qry, 0, keepdims=False)
    score_grad = (
        jnp.exp(scores - row_max[:, None]) / row_total[:, None] - target.astype(jnp.float32)
    ).astype(jnp.bfloat16)
    all_grad = lax.all_gather(score_grad, "k", axis=0, tiled=True)

    query_part = lax.dot_general(
        all_grad, passages, (((1,), (1,)), ((), ())), preferred_element_type=jnp.float32
    )
    query_part = lax.psum_scatter(query_part, QRY, scatter_dimension=1, tiled=True)
    query_part = lax.psum_scatter(query_part, "xh", scatter_dimension=0, tiled=True)
    query_piece = (query_part * score_scale).astype(jnp.bfloat16)
    query_grad = lax.all_gather(query_piece, "k", axis=1, tiled=True)
    query_grad = lax.all_gather(query_grad, ("y", "xh"), axis=0, tiled=True)

    sums = book_sums(codes, queries, all_grad).astype(jnp.bfloat16)
    sums = lax.psum_scatter(sums, QRY, scatter_dimension=0, tiled=True)
    sums = lax.psum(sums, ("xh", "y"))
    sums = lax.all_gather(sums, "k", axis=0, tiled=True)
    codebook_grad = unfold(sums.astype(jnp.float32))

    weight_grad = lax.dot_general(
        normed, query_grad, (((0,), (0,)), ((), ())), preferred_element_type=jnp.float32
    )
    norm_part = lax.dot_general(
        query_grad, proj_weight, (((1,), (1,)), ((), ())), preferred_element_type=jnp.float32
    ).astype(jnp.bfloat16)
    blocks = lax.all_to_all(
        norm_part.reshape(8, own_rows, row_span), QRY, split_axis=0, concat_axis=0, tiled=True
    )
    norm_piece = jnp.sum(blocks.astype(jnp.float32), axis=0).astype(jnp.bfloat16)
    norm_back = lax.all_gather(norm_piece, PSG, axis=1, tiled=True).astype(jnp.float32)
    scaled = norm_back * norm_gain[None, :]
    hidden_grad = (
        inverse * scaled
        - floats
        * inverse
        * inverse
        * inverse
        * jnp.mean(scaled * floats, axis=1, keepdims=True)
    ).astype(jnp.bfloat16)
    return (losses, hidden_grad, weight_grad, codebook_grad)


def solution(mesh):
    split = Mesh(mesh.devices.reshape(2, 4, 2, 4, 2), AXES)
    return jax.shard_map(
        per_device,
        mesh=split,
        in_specs=(P(QRY, None), P(), P(PSG, QRY), P(PSG, QRY), P(QRY, None, None), P()),
        out_specs=(P(QRY), P(QRY, None), P(PSG, QRY), P(QRY, None, None)),
        check_vma=False,
    )
```

time: 854 us -> 599 us (0.70)
  waiting for transfers between devices: 599 us -> 367 us
  matrix products: 102 us -> 20.3 us
  Pallas kernels: 0 us -> 59.2 us
  blocking collectives: 91.8 us -> 108 us
  other arithmetic: 29.4 us -> 17.1 us
  local copies, waits for them, and re-layouts: 15.8 us -> 6.67 us
    all_gather x3 -> x6, waiting for transfers between devices: 269 us -> 132 us  [the longest x1 40.3 us: per_device(): book = lax.all_gather(book_half, QRY, axis=0, tiled=True)]
    reduce_scatter x3 -> x7, waiting for transfers between devices: 284 us -> 167 us  [the longest x1 53.4 us: per_device(): lax.psum_scatter(query_part, QRY, scatter_dimension=1, tiled=True)]
    all_gather x0 -> x6, blocking collectives: none -> 90.1 us  [the longest x1 32.8 us: per_device(): lax.all_gather(jnp.stack([local_max, local_total, positive_part]), ('xh',...]
    dot_general x14 -> x5, matrix products: 102 us -> 20.3 us  [the longest x1 7.44 us: per_device(): lax.dot_general(all_grad, passages, (((1,), (1,)), ((), ())), preferred_e...]
    psum x1 -> x0, blocking collectives: 77.4 us -> none  [per_device(): query_grad = lax.psum(query_part, 'psg').astype(jnp.bfloat16)]
    pallas_call x0 -> x2, Pallas kernels: none -> 59.2 us  [the longest x1 43.3 us: book_sums(): pl.pallas_call(book_kernel, grid=(subs // 32,), in_specs=[pl.BlockSpec((3...]
    psum x1, waiting for transfers between devices: 44.1 us -> 67.4 us  [per_device(): sums = lax.psum(sums, ('xh', 'y'))]
    convert_element_type x4 -> x6, other arithmetic: 15.7 us -> 6.27 us  [the longest x1 2.71 us: per_device(): sums = book_sums(codes, queries, all_grad).astype(jnp.bfloat16)]
  transfers between devices with their start and end apart: 7 -> 15, of which waited for: 7 -> 12; matrix products, arithmetic and copies ran while one was open for 8% -> 3% of each run, Pallas kernels for 0% -> 10%
where the time goes in v1:
time: 599 us; the launch traced here: 598 us
  waiting for transfers between devices  367 us (61%)
  blocking collectives  108 us (18%)
  Pallas kernels  59.2 us (10%)
  matrix products  20.3 us (3%)
  other arithmetic  17.1 us (3%)
  between operations  14.1 us (2%)
  local copies, waits for them, and re-layouts  6.67 us (1%)
    psum x1, waiting for transfers between devices, per_device(): sums = lax.psum(sums, ('xh', 'y'))  67.4 us
    reduce_scatter x1, waiting for transfers between devices, per_device(): lax.psum_scatter(query_part, QRY, scatter_dimension=1, tiled=True)  53.4 us
    pallas_call x1, Pallas kernels, book_sums(): pl.pallas_call(book_kernel, grid=(subs // 32,), in_specs=[pl.BlockSpec((3...  43.3 us
    all_gather x1, waiting for transfers between devices, per_device(): book = lax.all_gather(book_half, QRY, axis=0, tiled=True)  40.3 us
    all_gather x1, waiting for transfers between devices, per_device(): lax.all_gather(norm_piece, PSG, axis=1, tiled=True).astype(jnp.float32)  34.7 us
    reduce_scatter x1, waiting for transfers between devices, per_device(): sums = lax.psum_scatter(sums, QRY, scatter_dimension=0, tiled=True)  34.1 us
    all_gather x1, blocking collectives, per_device(): lax.all_gather(jnp.stack([local_max, local_total, positive_part]), ('xh',...  32.8 us
    all_gather x1, blocking collectives, per_device(): normed = lax.all_gather(slice_own, QRY, axis=0, tiled=True)  26.5 us
  transfers between devices with their start and end apart: 15, of which 12 were waited for; matrix products, arithmetic and copies ran while one was open for 3% of the time, Pallas kernels for 10%

profile of v1, /device:TPU:1, one launch (start us, length us, event | category | flops | bytes accessed | tf_op | source)
XLA Modules:
  0.0 597.5 jit_solution(18172297014972456274)
XLA Ops:
  10.4 26.5 %all_gather.40 = bf16[1024,256]{1,0:T(8,128)(2,1)S(1)} all-gather(bf16[128,256]{1,0:T(8,128)(2,1)S(1)} %fusion.2), channel_id=1, replica_groups=mesh['xh'=2,'y'=4,'k'=2,'z'=4,'xl'=2] {'z','xl'}, dimensions={0}, use_global_device_ids=true | all-gather | bytes 589824 | tf_op jit(solution)/shard_map/all_gather | solution.py:101
  36.9 1.8 fusion.7
  38.8 19.1 %reduce-scatter.8.cloned.1.call-done = f32[1024,256]{1,0:T(8,128)} async-done(((f32[1024,512]{1,0:T(8,128)}), f32[1024,256]{1,0:T(8,128)}) %reduce-scatter.8.cloned.1.call-update) | async-done | bytes 1048592 | tf_op jit(solution)/shard_map/reduce_scatter | solution.py:113
  58.0 25.8 %reduce-scatter.10.cloned.1.call-done = f32[256,256]{1,0:T(8,128)} async-done(((f32[1024,256]{1,0:T(8,128)}), f32[256,256]{1,0:T(8,128)}) %reduce-scatter.10.cloned.1.call-update) | async-done | bytes 262160 | tf_op jit(solution)/shard_map/reduce_scatter | solution.py:114
  83.9 11.0 %all_to_all.36 = bf16[64,8,256]{2,0,1:T(8,128)(2,1)S(1)} all-to-all(bf16[64,8,256]{2,0,1:T(8,128)(2,1)S(1)} %bitcast.50), channel_id=1, replica_groups=mesh['xh'=2,'y'=4,'k'=2,'z'=4,'xl'=2] {'z','xl'}, dimensions={1} | all-to-all | bytes 524288 | tf_op jit(solution)/shard_map/all_to_all | solution.py:104
  94.9 7.2 %all_to_all.37 = bf16[2,256,256]{2,1,0:T(8,128)(2,1)S(1)} all-to-all(bf16[2,256,256]{2,1,0:T(8,128)(2,1)S(1)} %bitcast.52), channel_id=1, replica_groups=mesh['xh'=2,'y'=4,'k'=2,'z'=4,'xl'=2] {'k'}, dimensions={0} | all-to-all | bytes 524288 | tf_op jit(solution)/shard_map/all_to_all | solution.py:106
  104.9 5.4 all_gather.41
  110.4 16.3 %all-gather.13.cloned.1.call-done.codes_ref = bf16[256,2048]{1,0:T(8,128)(2,1)} async-done(((bf16[256,512]{1,0:T(8,128)(2,1)}), bf16[256,2048]{1,0:T(8,128)(2,1)}) %all-gather.13.cloned.1.call-update) | async-done | bytes 1048592 | tf_op jit(solution)/shard_map/all_gather | solution.py:107
  126.7 40.3 %all-gather.15.cloned.1.call-done.book_ref = bf16[2048,256]{1,0:T(8,128)(2,1)} async-done(((bf16[256,256]{1,0:T(8,128)(2,1)}), bf16[2048,256]{1,0:T(8,128)(2,1)}) %all-gather.15.cloned.1.call-update) | async-done | bytes 1048592 | tf_op jit(solution)/shard_map/all_gather | solution.py:109
  167.0 15.9 %decode.1 = bf16[2048,2048]{1,0:T(8,128)(2,1)} custom-call(bf16[256,2048]{1,0:T(8,128)(2,1)} %all-gather.13.cloned.1.call-done.codes_ref, bf16[2048,256]{1,0:T(8,128)(2,1)} %all-gather.15.cloned.1.call-done.book_ref), custom_call_target="tpu_custom_call" | custom-call | tf_op jit(solution)/shard_map/decode/pallas_call | solution.py:34
  182.9 25.3 %all-gather.11.cloned.1.call-done.queries_ref = bf16[256,2048]{1,0:T(8,128)(2,1)} async-done(((bf16[256,256]{1,0:T(8,128)(2,1)}), bf16[256,2048]{1,0:T(8,128)(2,1)}) %all-gather.11.cloned.1.call-update) | async-done | bytes 1048592 | tf_op jit(solution)/shard_map/all_gather | solution.py:117
  208.1 7.4 %fusion.8 = f32[256,2048]{1,0:T(8,128)} fusion(bf16[256,2048]{1,0:T(8,128)(2,1)} %all-gather.11.cloned.1.call-done.queries_ref, bf16[2048,2048]{1,0:T(8,128)(2,1)} %decode.1), kind=kOutput, calls=%fused_computation.47 | convolution fusion | flops 2147483648 | bytes 11534336 | tf_op jit(solution)/shard_map/dot_general | solution.py:119
  216.4 17.9 %reduce-scatter.14.cloned.1.call-done = f32[128,2048]{1,0:T(8,128)} async-done(((f32[256,2048]{1,0:T(8,128)}), f32[128,2048]{1,0:T(8,128)}) %reduce-scatter.14.cloned.1.call-update) | async-done | bytes 1048592 | tf_op jit(solution)/shard_map/reduce_scatter | solution.py:120
  235.7 1.7 exponential_reduce_fusion
  237.4 32.8 %all-gather.2 = f32[16,3,128]{2,1,0:T(4,128)S(1)} all-gather(f32[1,3,128]{2,1,0:T(4,128)S(1)} %maximum_bitcast_fusion), channel_id=2, replica_groups=mesh['xh'=2,'y'=4,'k'=2,'z'=4,'xl'=2] {'xh','z','xl'}, dimensions={0}, use_global_device_ids=true | all-gather | bytes 26112 | tf_op jit(solution)/shard_map/all_gather | solution.py:133
  271.6 15.2 %all-gather.17.cloned.1.call-done.sg_ref = bf16[256,2048]{1,0:T(8,128)(2,1)} async-done(((bf16[128,2048]{1,0:T(8,128)(2,1)}), bf16[256,2048]{1,0:T(8,128)(2,1)}) %all-gather.17.cloned.1.call-update) | async-done | bytes 1048592 | tf_op jit(solution)/shard_map/all_gather | solution.py:145
  286.7 7.4 %fusion.9 = f32[256,2048]{1,0:T(8,128)} fusion(bf16[256,2048]{1,0:T(8,128)(2,1)} %all-gather.17.cloned.1.call-done.sg_ref, bf16[2048,2048]{1,0:T(8,128)(2,1)} %decode.1), kind=kOutput, calls=%fused_computation.48 | convolution fusion | flops 2147483648 | bytes 11534336 | tf_op jit(solution)/shard_map/dot_general | solution.py:147
  294.3 53.4 %reduce-scatter.16.cloned.1.call-done = f32[256,256]{1,0:T(8,128)} async-done(((f32[256,2048]{1,0:T(8,128)}), f32[256,256]{1,0:T(8,128)}) %reduce-scatter.16.cloned.1.call-update) | async-done | bytes 262160 | tf_op jit(solution)/shard_map/reduce_scatter | solution.py:150
  347.7 17.2 %reduce-scatter.18.cloned.1.call-done = f32[128,256]{1,0:T(8,128)} async-done(((f32[256,256]{1,0:T(8,128)}), f32[128,256]{1,0:T(8,128)}) %reduce-scatter.18.cloned.1.call-update) | async-done | bytes 131088 | tf_op jit(solution)/shard_map/reduce_scatter | solution.py:151
  365.8 2.5 all_gather.49
  368.6 43.3 %book_sums.1 = f32[32,64,256]{2,1,0:T(8,128)} custom-call(bf16[256,2048]{1,0:T(8,128)(2,1)} %all-gather.13.cloned.1.call-done.codes_ref, bf16[256,2048]{1,0:T(8,128)(2,1)} %all-gather.11.cloned.1.call-done.queries_ref, bf16[256,2048]{1,0:T(8,128)(2,1)} %all-gather.17.cloned.1.call-done.sg_ref), custom_call_target="tpu_custom_call" | custom-call | tf_op jit(solution)/shard_map/book_sums/pallas_call | solution.py:69
  412.0 2.7 convert_element_type.50
  414.7 2.5 convolution_convert_fusion
  417.2 4.2 all-to-all-start.2
  421.4 34.1 %reduce-scatter.20.cloned.1.call-done = bf16[4,64,256]{2,1,0:T(8,128)(2,1)} async-done(((bf16[32,64,256]{2,1,0:T(8,128)(2,1)}), bf16[4,64,256]{2,1,0:T(8,128)(2,1)}) %reduce-scatter.20.cloned.1.call-update) | async-done | bytes 131088 | tf_op jit(solution)/shard_map/reduce_scatter | solution.py:157
  456.3 14.6 %all-gather.3 = f32[8,1,128]{2,1,0:T(1,128)S(1)} all-gather(f32[1,1,128]{2,1,0:T(1,128)S(1)} %subtract_bitcast_fusion), channel_id=3, replica_groups=mesh['xh'=2,'y'=4,'k'=2,'z'=4,'xl'=2] {'y','k'}, dimensions={0}, use_global_device_ids=true | all-gather | bytes 4608 | tf_op jit(solution)/shard_map/all_gather | solution.py:140
  471.5 67.4 %all-reduce.2.cloned.1.call-done = bf16[4,64,256]{2,1,0:T(8,128)(2,1)} async-done(((bf16[4,64,256]{2,1,0:T(8,128)(2,1)}), bf16[4,64,256]{2,1,0:T(8,128)(2,1)}) %all-reduce.2.cloned.1.call-update) | async-done | bytes 131088 | tf_op jit(solution)/shard_map/psum | solution.py:158
  538.8 8.2 %all_gather.52 = bf16[8,64,256]{2,1,0:T(8,128)(2,1)S(1)} all-gather(bf16[4,64,256]{2,1,0:T(8,128)(2,1)} %all-reduce.2.cloned.1.call-done), channel_id=1, replica_groups=mesh['xh'=2,'y'=4,'k'=2,'z'=4,'xl'=2] {'k'}, dimensions={0}, use_global_device_ids=true | all-gather | bytes 393216 | tf_op jit(solution)/shard_map/all_gather | solution.py:159
  548.8 2.7 reshape.85
  552.8 34.7 %all-gather.21.cloned.1.call-done = bf16[128,4096]{1,0:T(8,128)(2,1)} async-done(((bf16[128,256]{1,0:T(8,128)(2,1)}), bf16[128,4096]{1,0:T(8,128)(2,1)}) %all-gather.21.cloned.1.call-update) | async-done | bytes 1048592 | tf_op jit(solution)/shard_map/all_gather | solution.py:172
  587.5 1.7 fusion.1
  589.3 1.7 subtract_convert_fusion
  (74 shorter events, 15.5 us)
Async XLA Ops:
  7.2 29.8 %copy-start = (bf16[256,512]{1,0:T(8,128)(2,1)S(1)}, bf16[256,512]{1,0:T(8,128)(2,1)}, u32[]{:S(2)}) copy-start(bf16[256,512]{1,0:T(8,128)(2,1)} %param.8) | copy-start | bytes 786436
  7.2 50.7 %reduce-scatter.8.cloned.1.call-start = ((), (), s32[]{:S(2)}) async-start(), calls=%async_computation.10 | async-start | bytes 3145728 | tf_op jit(solution)/shard_map/reduce_scatter | solution.py:113
  7.2 3.0 copy-start.6
  38.7 45.1 %copy-start.5 = (s32[2048,64]{0,1:T(8,128)S(1)}, s32[2048,64]{0,1:T(8,128)}, u32[]{:S(2)}) copy-start(s32[2048,64]{0,1:T(8,128)} %param.9) | copy-start | bytes 1572868
  38.7 45.0 %reduce-scatter.10.cloned.1.call-start = ((), (), s32[]{:S(2)}) async-start(), calls=%async_computation.11 | async-start | bytes 1310720 | tf_op jit(solution)/shard_map/reduce_scatter | solution.py:114
  57.9 46.1 %reduce-scatter.12.cloned.1.call-start = ((), (), s32[]{:S(2)}) async-start(), calls=%async_computation.12 | async-start | bytes 393216 | tf_op jit(solution)/shard_map/reduce_scatter | solution.py:115
  83.8 19.5 %copy-start.7 = (bf16[64,8,256]{2,1,0:T(8,128)(2,1)S(1)}, bf16[64,8,256]{2,1,0:T(8,128)(2,1)}, u32[]{:S(2)}) copy-start(bf16[64,8,256]{2,1,0:T(8,128)(2,1)} %param.10) | copy-start | bytes 786436
  83.8 42.9 %all-gather.13.cloned.1.call-start = ((), (), s32[]{:S(2)}) async-start(), calls=%async_computation.14 | async-start | bytes 1310720 | tf_op jit(solution)/shard_map/all_gather | solution.py:107
  103.2 63.8 %all-gather.15.cloned.1.call-start = ((), (), s32[]{:S(2)}) async-start(), calls=%async_computation.15 | async-start | bytes 1179648 | tf_op jit(solution)/shard_map/all_gather | solution.py:109
  103.9 104.2 %all-gather.11.cloned.1.call-start = ((), (), s32[]{:S(2)}) async-start(), calls=%async_computation.13 | async-start | bytes 1179648 | tf_op jit(solution)/shard_map/all_gather | solution.py:117
  110.3 123.9 %reduce-scatter.14.cloned.1.call-start = ((), (), s32[]{:S(2)}) async-start(), calls=%async_computation.16 | async-start | bytes 3145728 | tf_op jit(solution)/shard_map/reduce_scatter | solution.py:120
  215.5 71.2 %all-gather.17.cloned.1.call-start = ((), (), s32[]{:S(2)}) async-start(), calls=%async_computation.17 | async-start | bytes 1572864 | tf_op jit(solution)/shard_map/all_gather | solution.py:145
  234.3 36.1 %copy-start.2 = (f32[128,2048]{1,0:T(8,128)S(1)}, f32[128,2048]{1,0:T(8,128)}, u32[]{:S(2)}) copy-start(f32[128,2048]{1,0:T(8,128)} %reduce-scatter.14.cloned.1.call-done) | copy-start | bytes 3145732
  271.5 76.1 %reduce-scatter.16.cloned.1.call-start = ((), (), s32[]{:S(2)}) async-start(), calls=%async_computation.18 | async-start | bytes 2359296 | tf_op jit(solution)/shard_map/reduce_scatter | solution.py:150
  294.2 70.7 %reduce-scatter.18.cloned.1.call-start = ((), (), s32[]{:S(2)}) async-start(), calls=%async_computation.19 | async-start | bytes 393216 | tf_op jit(solution)/shard_map/reduce_scatter | solution.py:151
  347.7 67.0 %all-gather.19.cloned.1.call-start = ((), (), s32[]{:S(2)}) async-start(), calls=%async_computation.20 | async-start | bytes 1179648 | tf_op jit(solution)/shard_map/all_gather | solution.py:154
  368.4 87.1 %reduce-scatter.20.cloned.1.call-start = ((), (), s32[]{:S(2)}) async-start(), calls=%async_computation.22 | async-start | bytes 1179648 | tf_op jit(solution)/shard_map/reduce_scatter | solution.py:157
  417.2 38.4 %all-to-all-start.2 = ((bf16[8,128,256]{2,1,0:T(8,128)(2,1)}), bf16[8,128,256]{2,1,0:T(8,128)(2,1)S(1)}, u32[]{:S(2)}, u32[]{:S(2)}) async-start(bf16[8,128,256]{2,1,0:T(8,128)(2,1)} %bitcast.16), calls=%async_computation.8 | async-start | bytes 1048576 | tf_op jit(solution)/shard_map/all_to_all | solution.py:168
  421.4 117.5 %all-reduce.2.cloned.1.call-start = ((), (), s32[]{:S(2)}) async-start(), calls=%async_computation.23 | async-start | bytes 262144 | tf_op jit(solution)/shard_map/psum | solution.py:158
  455.5 132.0 %all-gather.21.cloned.1.call-start = ((), (), s32[]{:S(2)}) async-start(), calls=%async_computation.21 | async-start | bytes 1114112 | tf_op jit(solution)/shard_map/all_gather | solution.py:172
  547.5 4.1 copy-start.3
  548.8 38.7 %copy-start.1 = (bf16[128,4096]{1,0:T(8,128)(2,1)S(1)}, bf16[128,4096]{1,0:T(8,128)(2,1)}, u32[]{:S(2)}) copy-start(bf16[128,4096]{1,0:T(8,128)(2,1)} %param.6) | copy-start | bytes 3145732
  587.5 1.7 copy-start.4
Sparse Core Ops, SparseCore 0:
  38.9 18.9 reduce-scatter.7
  60.3 23.4 reduce-scatter.9
  86.1 16.7 reduce-scatter.11
  105.0 21.6 all-gather.12
  128.7 38.1 all-gather.14
  168.4 39.6 all-gather.10
  215.7 18.5 reduce-scatter.13
  271.7 15.0 all-gather.16
  294.3 53.2 reduce-scatter.15
  349.8 15.0 reduce-scatter.17
  368.5 43.7 all-gather.18
  415.1 40.3 reduce-scatter.19
  458.0 80.8 all-reduce.1
  541.0 46.5 all-gather.20

commit v2 on v1

--- a/solution.py
+++ b/solution.py
@@ -77,6 +77,616 @@
     )(codes, queries, sg)
 
 
+def ring(c, step):
+    return lax.rem(c + (step + 4), 4)
+
+
+class Place:
+    def __init__(self):
+        self.xh, self.y, self.k, self.z, self.xl = (lax.axis_index(a) for a in AXES)
+        self.x = self.xh * 2 + self.xl
+        self.qry = self.z * 2 + self.xl
+
+    def along_x(self, step):
+        x = ring(self.x, step)
+        return {"xh": lax.div(x, 2), "xl": lax.rem(x, 2)}
+
+    def along_y(self, step):
+        return {"y": ring(self.y, step)}
+
+    def along_z(self, step):
+        return {"z": ring(self.z, step)}
+
+    def core(self):
+        return {"k": 1 - self.k}
+
+    def far_x(self):
+        return {"xh": 1 - self.xh}
+
+    def group(self):
+        return [
+            {"z": ring(self.z, s), "xl": lax.rem(self.xl + f, 2)}
+            for s in range(4)
+            for f in range(2)
+            if s or f
+        ]
+
+
+def greet(peers):
+    barrier = pltpu.get_barrier_semaphore()
+    for peer in peers:
+        pl.semaphore_signal(
+            barrier, inc=1, device_id=peer, device_id_type=pl.DeviceIdType.MESH
+        )
+    pl.semaphore_wait(barrier, len(peers))
+
+
+class Wires:
+    def __init__(self, send_sems, recv_sems):
+        self.send_sems, self.recv_sems, self.copies = send_sems, recv_sems, []
+
+    def send(self, src, dst, peer):
+        n = len(self.copies)
+        copy = pltpu.make_async_remote_copy(
+            src_ref=src,
+            dst_ref=dst,
+            send_sem=self.send_sems.at[n],
+            recv_sem=self.recv_sems.at[n],
+            device_id=peer,
+            device_id_type=pl.DeviceIdType.MESH,
+        )
+        copy.start()
+        self.copies.append(copy)
+        return copy
+
+    def drain(self):
+        for copy in self.copies:
+            copy.wait_send()
+
+
+def ring_gather(wires, along, own, block, halves):
+    first = (wires.send(own, block(0), along(1)), wires.send(own, block(0), along(-1)))
+
+    def forward():
+        first[0].wait_recv()
+        up = wires.send(halves(block(-1), 0), halves(block(-1), 0), along(1))
+        first[1].wait_recv()
+        down = wires.send(halves(block(1), 1), halves(block(1), 1), along(-1))
+
+        def finish():
+            up.wait_recv()
+            down.wait_recv()
+
+        return finish
+
+    return forward
+
+
+def torus_gather(wires, one, two, own, block, halves):
+    forward = ring_gather(wires, one, own, lambda i: block(i, 0), halves)
+    rest = [ring_gather(wires, two, own, lambda j: block(0, j), halves)]
+    yield
+    finish = forward()
+    for i in (-1, 1):
+        rest.append(
+            ring_gather(wires, two, block(i, 0), lambda j, i=i: block(i, j), halves)
+        )
+    yield
+    ends = [rest[0]()]
+    finish()
+    rest.append(ring_gather(wires, two, block(2, 0), lambda j: block(2, j), halves))
+    yield
+    ends += [r() for r in rest[1:3]]
+    yield
+    ends.append(rest[3]())
+    for end in ends:
+        end()
+
+
+def run_together(*parts):
+    live = list(parts)
+    while live:
+        live = [p for p in live if next(p, live) is not live]
+
+
+def both(*parts):
+    live = list(parts)
+    while live:
+        live = [p for p in live if next(p, live) is not live]
+        yield
+
+
+def psg_gather(wires, at, own, block):
+    def halves(ref, side):
+        rows = ref.shape[0] // 2
+        return ref.at[rows * side : rows * side + rows]
+
+    def near(s):
+        return block(at.xh, ring(at.y, s), at.k)
+
+    def far(s):
+        return block(1 - at.xh, ring(at.y, s), at.k)
+
+    across = wires.send(own, near(0), at.far_x())
+    forward = ring_gather(wires, at.along_y, own, near, halves)
+    cores = [wires.send(own, near(0), at.core())]
+    yield
+    across.wait_recv()
+    forward_far = ring_gather(wires, at.along_y, far(0), far, halves)
+    cores.append(wires.send(far(0), far(0), at.core()))
+    yield
+    finish = forward()
+    for s in (-1, 1):
+        cores.append(wires.send(near(s), near(s), at.core()))
+    yield
+    finish_far = forward_far()
+    for s in (-1, 1):
+        cores.append(wires.send(far(s), far(s), at.core()))
+    yield
+    finish()
+    cores.append(wires.send(near(2), near(2), at.core()))
+    finish_far()
+    cores.append(wires.send(far(2), far(2), at.core()))
+    for copy in cores:
+        copy.wait_recv()
+
+
+def rows_half(ref, side):
+    rows = ref.shape[-2] // 2
+    return ref.at[rows * side : rows * side + rows]
+
+
+def exchange_kernel(
+    slice_ref, weight_ref, codes_ref, book_ref,
+    normed_ref, queries_ref, codes_all_ref, book_all_ref,
+    other_ref, came_ref, acc_ref, up_ref, down_ref, from_up_ref, from_down_ref, far_ref, piece_ref,
+    send_sems, recv_sems,
+):
+    at = Place()
+    wires = Wires(send_sems, recv_sems)
+    group = at.group()
+    greet(
+        group
+        + [{"k": 1 - at.k, **g} for g in group]
+        + [at.core(), at.along_y(1), at.along_y(-1), at.far_x()]
+        + [{"xh": 1 - at.xh, "xl": 1 - at.xl}]
+    )
+    sent = []
+    mine = pl.ds(pl.multiple_of(at.y * 512 + at.k * 256, 256), 256)
+    rows_here = pl.ds(pl.multiple_of(at.qry * 32, 32), 32)
+    for cross in range(2):
+        k = at.k if cross == 0 else 1 - at.k
+        rows_there = pl.ds(pl.multiple_of(k * 32, 32), 32)
+        for peer in ([] if cross == 0 else [{}]) + group:
+            q = peer["z"] * 2 + peer["xl"] if peer else at.qry
+            sent.append(
+                wires.send(
+                    codes_ref.at[rows_there, pl.ds(pl.multiple_of(q * 256, 256), 256)],
+                    codes_all_ref.at[rows_here, mine],
+                    {"k": k, **peer},
+                )
+            )
+    codes_all_ref[rows_here, mine] = codes_ref[
+        pl.ds(pl.multiple_of(at.k * 32, 32), 32),
+        pl.ds(pl.multiple_of(at.qry * 256, 256), 256),
+    ]
+
+    def column(ref, flip):
+        return lambda s: ref.at[ring(at.z, s) * 2 + (at.xl if flip == 0 else 1 - at.xl)]
+
+    partner = {"xl": 1 - at.xl}
+    gathers = []
+    for own, out in ((slice_ref, normed_ref), (book_ref, book_all_ref)):
+        side = wires.send(own, out.at[at.qry], partner)
+        gathers.append((side, out, ring_gather(wires, at.along_z, own, column(out, 0), rows_half)))
+    normed_ref[at.qry] = slice_ref[...]
+    book_all_ref[at.qry] = book_ref[...]
+    ends = []
+    for side, out, forward in gathers:
+        side.wait_recv()
+        far = column(out, 1)
+        second = ring_gather(wires, at.along_z, far(0), far, rows_half)
+        ends.append((forward(), second))
+    normed_end = ends[0][1]()
+    ends[0][0]()
+    normed_end()
+
+    order = (2, 1, -1, 0)
+    crossed = []
+    for s in order:
+        b = ring(at.y, s)
+        left = normed_ref[pl.ds(b * 2, 2)].reshape(256, 256)
+        other_ref[b] = jnp.dot(
+            left,
+            weight_ref[:, pl.ds(pl.multiple_of((1 - at.k) * 256, 256), 256)],
+            preferred_element_type=jnp.float32,
+        )
+        crossed.append(wires.send(other_ref.at[b], came_ref.at[b], at.core()))
+    for s in order:
+        b = ring(at.y, s)
+        left = normed_ref[pl.ds(b * 2, 2)].reshape(256, 256)
+        acc_ref[b] = jnp.dot(
+            left,
+            weight_ref[:, pl.ds(pl.multiple_of(at.k * 256, 256), 256)],
+            preferred_element_type=jnp.float32,
+        )
+    far_y, next_y, last_y = ring(at.y, 2), ring(at.y, 1), ring(at.y, -1)
+    crossed[0].wait_recv()
+    acc_ref[far_y] = acc_ref[far_y] + came_ref[far_y]
+    up = wires.send(acc_ref.at[far_y, 0:128], up_ref, at.along_y(1))
+    down = wires.send(acc_ref.at[far_y, 128:256], down_ref, at.along_y(-1))
+    crossed[1].wait_recv()
+    acc_ref[next_y] = acc_ref[next_y] + came_ref[next_y]
+    crossed[2].wait_recv()
+    acc_ref[last_y] = acc_ref[last_y] + came_ref[last_y]
+    crossed[3].wait_recv()
+    acc_ref[at.y] = acc_ref[at.y] + came_ref[at.y]
+    up.wait_recv()
+    acc_ref[next_y, 0:128] = acc_ref[next_y, 0:128] + up_ref[...]
+    up = wires.send(acc_ref.at[next_y], from_up_ref, at.along_y(1))
+    down.wait_recv()
+    acc_ref[last_y, 128:256] = acc_ref[last_y, 128:256] + down_ref[...]
+    down = wires.send(acc_ref.at[last_y], from_down_ref, at.along_y(-1))
+
+    for copy in sent:
+        copy.wait_recv()
+
+    def chunk(s):
+        return codes_all_ref.at[:, pl.ds(pl.multiple_of(ring(at.y, s) * 512, 512), 512)]
+
+    codes_forward = ring_gather(wires, at.along_y, chunk(0), chunk, rows_half)
+
+    up.wait_recv()
+    down.wait_recv()
+    acc_ref[at.y] = acc_ref[at.y] + from_up_ref[...] + from_down_ref[...]
+    far_rows = pl.ds(pl.multiple_of((1 - at.xh) * 128, 128), 128)
+    own_rows = pl.ds(pl.multiple_of(at.xh * 128, 128), 128)
+    across = wires.send(acc_ref.at[at.y, far_rows], far_ref, at.far_x())
+    across.wait_recv()
+    piece_ref[...] = (acc_ref[at.y, own_rows] + far_ref[...]).astype(jnp.bfloat16)
+
+    def spot(x, z):
+        q = z * 2 + lax.rem(x, 2)
+        return pl.multiple_of(lax.div(x, 2) * 128, 128), pl.ds(pl.multiple_of(q * 256, 256), 256)
+
+    def colour(n, x, z):
+        row, cols = spot(x, z)
+        return queries_ref.at[pl.ds(row + n * 64, 64), cols]
+
+    row, cols = spot(at.x, at.z)
+    queries_ref[pl.ds(row, 128), cols] = piece_ref[...]
+    run_together(
+        torus_gather(
+            wires, at.along_x, at.along_z, piece_ref.at[0:64],
+            lambda i, j: colour(0, ring(at.x, i), ring(at.z, j)), rows_half,
+        ),
+        torus_gather(
+            wires, at.along_z, at.along_x, piece_ref.at[64:128],
+            lambda i, j: colour(1, ring(at.x, j), ring(at.z, i)), rows_half,
+        ),
+    )
+    book_end = ends[1][1]()
+    ends[1][0]()
+    book_end()
+    codes_forward()()
+    wires.drain()
+
+
+VM = pl.BlockSpec(memory_space=pltpu.VMEM)
+
+
+def exchange(slice_own, weight, codes, book_half):
+    f32, b16 = jnp.float32, jnp.bfloat16
+    return pl.pallas_call(
+        exchange_kernel,
+        in_specs=[VM] * 4,
+        out_specs=[VM] * 4,
+        out_shape=[
+            jax.ShapeDtypeStruct((8, 128, 256), b16),
+            jax.ShapeDtypeStruct((256, 2048), b16),
+            jax.ShapeDtypeStruct((256, 2048), b16),
+            jax.ShapeDtypeStruct((8, 256, 256), b16),
+        ],
+        scratch_shapes=[
+            pltpu.VMEM((4, 256, 256), f32),
+            pltpu.VMEM((4, 256, 256), f32),
+            pltpu.VMEM((4, 256, 256), f32),
+            pltpu.VMEM((128, 256), f32),
+            pltpu.VMEM((128, 256), f32),
+            pltpu.VMEM((256, 256), f32),
+            pltpu.VMEM((256, 256), f32),
+            pltpu.VMEM((128, 256), f32),
+            pltpu.VMEM((128, 256), b16),
+            pltpu.SemaphoreType.DMA((96,)),
+            pltpu.SemaphoreType.DMA((96,)),
+        ],
+        compiler_params=pltpu.CompilerParams(collective_id=0, has_side_effects=True),
+        name="exchange",
+    )(slice_own, weight, codes, book_half)
+
+
+def scores_kernel(
+    queries_ref, passages_ref, column_ref, all_grad_ref, losses_ref,
+    other_ref, came_ref, scores_ref, stat_ref, stats_ref, grad_ref,
+    send_sems, recv_sems,
+):
+    at = Place()
+    wires = Wires(send_sems, recv_sems)
+    cells = [
+        {"xh": lax.rem(at.xh + h, 2), **({} if not g else g)}
+        for h in range(2)
+        for g in [None] + at.group()
+        if h or g
+    ]
+    greet([at.core()] + cells)
+    there = pl.ds(pl.multiple_of((1 - at.k) * 128, 128), 128)
+    here = pl.ds(pl.multiple_of(at.k * 128, 128), 128)
+    parts = 4
+    width = passages_ref.shape[1] // parts
+    crossed = []
+    for part in range(parts):
+        cols = slice(part * width, (part + 1) * width)
+        other_ref[:, cols] = jnp.dot(
+            queries_ref[there, :], passages_ref[:, cols], preferred_element_type=jnp.float32
+        )
+        crossed.append(wires.send(other_ref.at[:, cols], came_ref.at[:, cols], at.core()))
+    for part in range(parts):
+        cols = slice(part * width, (part + 1) * width)
+        scores_ref[:, cols] = jnp.dot(
+            queries_ref[here, :], passages_ref[:, cols], preferred_element_type=jnp.float32
+        )
+    for copy in crossed:
+        copy.wait_recv()
+    scores = (scores_ref[...] + came_ref[...]) * score_scale
+    scores_ref[...] = scores
+    target = lax.broadcasted_iota(jnp.int32, scores.shape, 1) == column_ref[...]
+    local_max = jnp.max(scores, axis=1, keepdims=True)
+    positive = jnp.sum(jnp.where(target, scores, 0.0), axis=1, keepdims=True)
+    local_total = jnp.sum(jnp.exp(scores - local_max), axis=1, keepdims=True)
+    lane = lax.broadcasted_iota(jnp.int32, (128, 128), 1)
+    packed = jnp.where(lane == 0, local_max, jnp.where(lane == 1, local_total, positive))
+    mine = jnp.transpose(packed)[0:8, :]
+    stat_ref[...] = mine
+    slot = at.xh * 8 + at.qry
+    copies = [wires.send(stat_ref, stats_ref.at[slot], cell) for cell in cells]
+    stats_ref[slot] = mine
+    for copy in copies:
+        copy.wait_recv()
+    high = stats_ref[0, 0:1, :]
+    for n in range(1, 16):
+        high = jnp.maximum(high, stats_ref[n, 0:1, :])
+    total = jnp.zeros_like(high)
+    hit = jnp.zeros_like(high)
+    for n in range(16):
+        total = total + stats_ref[n, 1:2, :] * jnp.exp(stats_ref[n, 0:1, :] - high)
+        hit = hit + stats_ref[n, 2:3, :]
+    losses_ref[...] = jnp.broadcast_to(jnp.log(total) + high - hit, (8, 128))
+    row = lax.broadcasted_iota(jnp.int32, (128, 128), 0)
+    back = jnp.transpose(jnp.where(row == 0, high, total))
+    row_max, row_total = back[:, 0:1], back[:, 1:2]
+    grad = jnp.exp(scores_ref[...] - row_max) / row_total - target.astype(jnp.float32)
+    grad = grad.astype(jnp.bfloat16)
+    grad_ref[...] = grad
+    copy = wires.send(grad_ref, all_grad_ref.at[here], at.core())
+    all_grad_ref[here, :] = grad
+    copy.wait_recv()
+    wires.drain()
+
+
+def score_grads(queries, passages, column):
+    f32, b16 = jnp.float32, jnp.bfloat16
+    count = passages.shape[1]
+    return pl.pallas_call(
+        scores_kernel,
+        in_specs=[VM] * 3,
+        out_specs=[VM] * 2,
+        out_shape=[jax.ShapeDtypeStruct((256, count), b16), jax.ShapeDtypeStruct((8, 128), f32)],
+        scratch_shapes=[
+            pltpu.VMEM((128, count), f32),
+            pltpu.VMEM((128, count), f32),
+            pltpu.VMEM((128, count), f32),
+            pltpu.VMEM((8, 128), f32),
+            pltpu.VMEM((16, 8, 128), f32),
+            pltpu.VMEM((128, count), b16),
+            pltpu.SemaphoreType.DMA((24,)),
+            pltpu.SemaphoreType.DMA((24,)),
+        ],
+        compiler_params=pltpu.CompilerParams(collective_id=1, has_side_effects=True),
+        name="score_grads",
+    )(queries, passages, column)
+
+
+def ring_sum(wires, along, block, half, came):
+    def add(ref, *others):
+        total = ref[...].astype(jnp.float32)
+        for other in others:
+            total = total + other[...].astype(jnp.float32)
+        ref[...] = total.astype(ref.dtype)
+
+    up_half, down_half, up_full, down_full = came
+    up = wires.send(half(block(2), 0), up_half, along(1))
+    down = wires.send(half(block(2), 1), down_half, along(-1))
+    yield
+    up.wait_recv()
+    add(half(block(1), 0), up_half)
+    up = wires.send(block(1), up_full, along(1))
+    down.wait_recv()
+    add(half(block(-1), 1), down_half)
+    down = wires.send(block(-1), down_full, along(-1))
+    yield
+    up.wait_recv()
+    down.wait_recv()
+    add(block(0), up_full, down_full)
+
+
+def middle_half(ref, side):
+    rows = ref.shape[-2] // 2
+    return ref.at[:, rows * side : rows * side + rows]
+
+
+def grads_kernel(
+    grad_ref, passages_ref, normed_ref, weight_ref, losses_ref, sums_ref,
+    weight_grad_ref, norm_ref, losses_all_ref, book_ref,
+    part_ref, x_half, x_full, z_half, z_full, piece_ref, query_ref, term_ref, terms_ref, norm_piece_ref,
+    add_ref, y_half, y_full, share_ref, far_ref, final_ref,
+    send_sems, recv_sems,
+):
+    at = Place()
+    wires = Wires(send_sems, recv_sems)
+    group = at.group()
+    cells = [at.core()] + [{**at.along_y(s), "k": c} for s in (1, 2, 3) for c in (at.k, 1 - at.k)]
+    greet(group + cells + [at.far_x(), {"xh": 1 - at.xh, "xl": 1 - at.xl}])
+    places = at.y * 2 + at.k
+    lost = [wires.send(losses_ref, losses_all_ref.at[places], cell) for cell in cells]
+    losses_all_ref[places] = losses_ref[...]
+
+    def book_sums_over_devices():
+        add_ref[...] = sums_ref[...]
+        yield from ring_sum(
+            wires, at.along_y, lambda s: add_ref.at[ring(at.y, s)], middle_half,
+            (y_half.at[0], y_half.at[1], y_full.at[0], y_full.at[1]),
+        )
+        copies = []
+        for n, peer in enumerate(group):
+            q = peer["z"] * 2 + peer["xl"]
+            copies.append(wires.send(add_ref.at[at.y, q], share_ref.at[n], peer))
+        yield
+        total = add_ref[at.y, at.qry].astype(jnp.float32)
+        for n, copy in enumerate(copies):
+            copy.wait_recv()
+            total = total + share_ref[n].astype(jnp.float32)
+        final_ref[0] = total.astype(jnp.bfloat16)
+        across = wires.send(final_ref.at[0], far_ref, at.far_x())
+        yield
+        across.wait_recv()
+        whole = final_ref[0].astype(jnp.float32) + far_ref[...].astype(jnp.float32)
+        final_ref[1] = whole.astype(jnp.bfloat16)
+
+        def spot(s):
+            return book_ref.at[at.k, ring(at.y, s)]
+
+        forward = ring_gather(wires, at.along_y, final_ref.at[1], spot, rows_half)
+        cores = [wires.send(final_ref.at[1], spot(0), at.core())]
+        book_ref[at.k, at.y] = final_ref[1]
+        yield
+        finish = forward()
+        for s in (-1, 1):
+            cores.append(wires.send(spot(s), spot(s), at.core()))
+        yield
+        finish()
+        cores.append(wires.send(spot(2), spot(2), at.core()))
+        yield
+        for copy in cores:
+            copy.wait_recv()
+
+    def main():
+        for q in range(8):
+            product = lax.dot_general(
+                grad_ref[...], passages_ref[q * 256 : q * 256 + 256, :],
+                (((1,), (1,)), ((), ())), preferred_element_type=jnp.float32,
+            )
+            z, xl = divmod(q, 2)
+            for xh in range(2):
+                x = xh * 2 + xl
+                part_ref[0, x, z] = product[xh * 128 : xh * 128 + 128, 0:128]
+                part_ref[1, z, x] = product[xh * 128 : xh * 128 + 128, 128:256]
+        pair = [
+            ring_sum(
+                wires, along, lambda s, n=n, c=c: part_ref.at[n, ring(c, s)], middle_half,
+                (x_half.at[n, 0], x_half.at[n, 1], x_full.at[n, 0], x_full.at[n, 1]),
+            )
+            for n, along, c in ((0, at.along_x, at.x), (1, at.along_z, at.z))
+        ]
+        yield from both(*pair)
+        pair = [
+            ring_sum(
+                wires, along, lambda s, n=n, b=b, c=c: part_ref.at[n, b, ring(c, s)], rows_half,
+                (z_half.at[n, 0], z_half.at[n, 1], z_full.at[n, 0], z_full.at[n, 1]),
+            )
+            for n, along, b, c in ((0, at.along_z, at.x, at.z), (1, at.along_x, at.z, at.x))
+        ]
+        yield from both(*pair)
+        for n, b, c in ((0, at.x, at.z), (1, at.z, at.x)):
+            piece_ref[:, n * 128 : n * 128 + 128] = (part_ref[n, b, c] * score_scale).astype(jnp.bfloat16)
+
+        def spot(xh, y, k):
+            return query_ref.at[
+                pl.ds(pl.multiple_of(y * 256 + xh * 128, 128), 128),
+                pl.ds(pl.multiple_of(k * 256, 256), 256),
+            ]
+
+        spot(at.xh, at.y, at.k)[...] = piece_ref[...]
+        yield from psg_gather(wires, at, piece_ref, spot)
+        for q in range(8):
+            term_ref[q] = lax.dot_general(
+                query_ref[q * 128 : q * 128 + 128, :], weight_ref[...],
+                (((1,), (1,)), ((), ())), preferred_element_type=jnp.float32,
+            ).astype(jnp.bfloat16)
+        copies = []
+        for n, peer in enumerate(group):
+            q = peer["z"] * 2 + peer["xl"]
+            copies.append(wires.send(term_ref.at[q], terms_ref.at[n], peer))
+        weight_grad_ref[...] = lax.dot_general(
+            normed_ref[...].reshape(1024, 256), query_ref[...],
+            (((0,), (0,)), ((), ())), preferred_element_type=jnp.float32,
+        )
+        yield
+        total = term_ref[at.qry].astype(jnp.float32)
+        for n, copy in enumerate(copies):
+            copy.wait_recv()
+            total = total + terms_ref[n].astype(jnp.float32)
+        norm_piece_ref[...] = total.astype(jnp.bfloat16)
+
+        def column(xh, y, k):
+            place = (xh * 4 + y) * 2 + k
+            return norm_ref.at[:, pl.ds(pl.multiple_of(place * 256, 256), 256)]
+
+        column(at.xh, at.y, at.k)[...] = norm_piece_ref[...]
+        yield from psg_gather(wires, at, norm_piece_ref, column)
+
+    run_together(main(), book_sums_over_devices())
+    for copy in lost:
+        copy.wait_recv()
+    wires.drain()
+
+
+def grads(all_grad, passages, normed, weight, losses, sums):
+    f32, b16 = jnp.float32, jnp.bfloat16
+    return pl.pallas_call(
+        grads_kernel,
+        in_specs=[VM] * 6,
+        out_specs=[VM] * 4,
+        out_shape=[
+            jax.ShapeDtypeStruct((256, 512), f32),
+            jax.ShapeDtypeStruct((128, 4096), b16),
+            jax.ShapeDtypeStruct((8, 8, 128), f32),
+            jax.ShapeDtypeStruct((2, 4, 64, 256), b16),
+        ],
+        scratch_shapes=[
+            pltpu.VMEM((2, 4, 4, 128, 128), f32),
+            pltpu.VMEM((2, 2, 4, 64, 128), f32),
+            pltpu.VMEM((2, 2, 4, 128, 128), f32),
+            pltpu.VMEM((2, 2, 64, 128), f32),
+            pltpu.VMEM((2, 2, 128, 128), f32),
+            pltpu.VMEM((128, 256), b16),
+            pltpu.VMEM((1024, 512), b16),
+            pltpu.VMEM((8, 128, 256), b16),
+            pltpu.VMEM((7, 128, 256), b16),
+            pltpu.VMEM((128, 256), b16),
+            pltpu.VMEM((4, 8, 64, 256), b16),
+            pltpu.VMEM((2, 8, 32, 256), b16),
+            pltpu.VMEM((2, 8, 64, 256), b16),
+            pltpu.VMEM((7, 64, 256), b16),
+            pltpu.VMEM((64, 256), b16),
+            pltpu.VMEM((2, 64, 256), b16),
+            pltpu.SemaphoreType.DMA((112,)),
+            pltpu.SemaphoreType.DMA((112,)),
+        ],
+        compiler_params=pltpu.CompilerParams(collective_id=2, has_side_effects=True),
+        name="grads",
+    )(all_grad, passages, normed, weight, losses, sums)
+
+
 def unfold(sums):
     groups = sums.shape[0]
     parts = sums.reshape(groups, 64, 8, 4, 8)
@@ -98,26 +708,10 @@
     inverse = lax.rsqrt(jnp.mean(floats * floats, axis=1, keepdims=True) + norm_eps)
     normed_own = (floats * inverse * norm_gain[None, :]).astype(jnp.bfloat16)
     slice_own = lax.dynamic_slice_in_dim(normed_own, psg * row_span, row_span, 1)
-    normed = lax.all_gather(slice_own, QRY, axis=0, tiled=True)
-
     codes = pq_codes.T.astype(jnp.bfloat16)
-    codes = lax.all_to_all(codes, QRY, split_axis=1, concat_axis=0, tiled=True)
-    codes = codes.reshape(8, 2, half, piece).transpose(1, 0, 2, 3).reshape(2, 8 * half, piece)
-    codes = lax.all_to_all(codes, "k", split_axis=0, concat_axis=2, tiled=True)[0]
-    codes = lax.all_gather(codes, "y", axis=1, tiled=True)
     book_half = lax.dynamic_slice_in_dim(codebook, k * half, half, 0).reshape(half * 8, 256)
-    book = lax.all_gather(book_half, QRY, axis=0, tiled=True)
-    passages = decode(codes, book)
-
-    part = jnp.dot(normed, proj_weight, preferred_element_type=jnp.float32)
-    part = lax.psum_scatter(part, "k", scatter_dimension=1, tiled=True)
-    part = lax.psum_scatter(part, "y", scatter_dimension=0, tiled=True)
-    part = lax.psum_scatter(part, "xh", scatter_dimension=0, tiled=True)
-    queries = lax.all_gather(part.astype(jnp.bfloat16), "xh", axis=0, tiled=True)
-    queries = lax.all_gather(queries, QRY, axis=1, tiled=True)
-
-    partial_value = jnp.dot(queries, passages, preferred_element_type=jnp.float32)
-    scores = lax.psum_scatter(partial_value, "k", scatter_dimension=0, tiled=True) * score_scale
+    normed, queries, codes, book = exchange(slice_own, proj_weight, codes, book_half)
+    passages = decode(codes, book.reshape(2048, 256))
 
     block = y * 2 + k
     targets = lax.dynamic_slice_in_dim(positives, block * own_rows, own_rows, 0)
@@ -126,50 +720,15 @@
     sixth = inside // piece
     here = (shard // 8 == xh) & (sixth == qry)
     column = jnp.where(here, (shard % 8) * piece + inside % piece, -1)
-    target = lax.broadcasted_iota(jnp.int32, scores.shape, 1) == column[:, None]
-    local_max = jnp.max(scores, axis=1)
-    positive_part = jnp.sum(jnp.where(target, scores, 0.0), axis=1)
-    local_total = jnp.sum(jnp.exp(scores - local_max[:, None]), axis=1)
-    stats = lax.all_gather(
-        jnp.stack([local_max, local_total, positive_part]), ("xh", "z", "xl"), axis=0
+    all_grad, block_losses = score_grads(queries, passages, column[:, None])
+    sums = book_sums(codes, queries, all_grad).astype(jnp.bfloat16)
+    sums = sums.reshape(8, 4, 64, 256).transpose(1, 0, 2, 3)
+    weight_grad, norm_back, all_losses, book_grad = grads(
+        all_grad, passages, normed, proj_weight, block_losses, sums
     )
-    row_max = jnp.max(stats[:, 0], axis=0)
-    row_total = jnp.sum(stats[:, 1] * jnp.exp(stats[:, 0] - row_max[None, :]), axis=0)
-    positive_score = jnp.sum(stats[:, 2], axis=0)
-    block_losses = jnp.log(row_total) + row_max - positive_score
-    losses = lax.all_gather(block_losses, ("y", "k"), axis=0)
-    losses = lax.dynamic_index_in_dim(losses, qry, 0, keepdims=False)
-    score_grad = (
-        jnp.exp(scores - row_max[:, None]) / row_total[:, None] - target.astype(jnp.float32)
-    ).astype(jnp.bfloat16)
-    all_grad = lax.all_gather(score_grad, "k", axis=0, tiled=True)
-
-    query_part = lax.dot_general(
-        all_grad, passages, (((1,), (1,)), ((), ())), preferred_element_type=jnp.float32
-    )
-    query_part = lax.psum_scatter(query_part, QRY, scatter_dimension=1, tiled=True)
-    query_part = lax.psum_scatter(query_part, "xh", scatter_dimension=0, tiled=True)
-    query_piece = (query_part * score_scale).astype(jnp.bfloat16)
-    query_grad = lax.all_gather(query_piece, "k", axis=1, tiled=True)
-    query_grad = lax.all_gather(query_grad, ("y", "xh"), axis=0, tiled=True)
-
-    sums = book_sums(codes, queries, all_grad).astype(jnp.bfloat16)
-    sums = lax.psum_scatter(sums, QRY, scatter_dimension=0, tiled=True)
-    sums = lax.psum(sums, ("xh", "y"))
-    sums = lax.all_gather(sums, "k", axis=0, tiled=True)
-    codebook_grad = unfold(sums.astype(jnp.float32))
-
-    weight_grad = lax.dot_general(
-        normed, query_grad, (((0,), (0,)), ((), ())), preferred_element_type=jnp.float32
-    )
-    norm_part = lax.dot_general(
-        query_grad, proj_weight, (((1,), (1,)), ((), ())), preferred_element_type=jnp.float32
-    ).astype(jnp.bfloat16)
-    blocks = lax.all_to_all(
-        norm_part.reshape(8, own_rows, row_span), QRY, split_axis=0, concat_axis=0, tiled=True
-    )
-    norm_piece = jnp.sum(blocks.astype(jnp.float32), axis=0).astype(jnp.bfloat16)
-    norm_back = lax.all_gather(norm_piece, PSG, axis=1, tiled=True).astype(jnp.float32)
+    losses = lax.dynamic_index_in_dim(all_losses, qry, 0, keepdims=False)[0]
+    codebook_grad = unfold(book_grad.reshape(8, 64, 256).astype(jnp.float32))
+    norm_back = norm_back.astype(jnp.float32)
     scaled = norm_back * norm_gain[None, :]
     hidden_grad = (
         inverse * scaled

time: 599 us -> 243 us (0.41)
  waiting for transfers between devices: 367 us -> 0 us
  Pallas kernels: 59.2 us -> 224 us
  blocking collectives: 108 us -> 0 us
  matrix products: 20.3 us -> 0 us
  between operations: 14.1 us -> 0.77 us
  other arithmetic: 17.1 us -> 10.1 us
    reduce_scatter x7 -> x0, waiting for transfers between devices: 167 us -> none  [the longest x1 53.4 us: per_device(): lax.psum_scatter(query_part, QRY, scatter_dimension=1, tiled=True)]
    pallas_call x0 -> x3, Pallas kernels: none -> 164 us  [the longest x1 70.2 us: grads(): pl.pallas_call(grads_kernel, in_specs=[VM] * 6, out_specs=[VM] * 4, out_s...]
    all_gather x6 -> x0, waiting for transfers between devices: 132 us -> none  [the longest x1 40.3 us: per_device(): book = lax.all_gather(book_half, QRY, axis=0, tiled=True)]
    all_gather x6 -> x0, blocking collectives: 90.1 us -> none  [the longest x1 32.8 us: per_device(): lax.all_gather(jnp.stack([local_max, local_total, positive_part]), ('xh',...]
    psum x1 -> x0, waiting for transfers between devices: 67.4 us -> none  [per_device(): sums = lax.psum(sums, ('xh', 'y'))]
    dot_general x5 -> x0, matrix products: 20.3 us -> none  [the longest x1 7.44 us: per_device(): lax.dot_general(all_grad, passages, (((1,), (1,)), ((), ())), preferred_e...]
    all_to_all x2 -> x0, blocking collectives: 18.2 us -> none  [the longest x1 11 us: per_device(): codes = lax.all_to_all(codes, QRY, split_axis=1, concat_axis=0, tiled=True)]
  transfers between devices with their start and end apart: 15 -> 0, of which waited for: 12 -> 0; matrix products, arithmetic and copies ran while one was open for 3% -> 0% of each run, Pallas kernels for 10% -> 0%
where the time goes in v2:
time: 243 us; the launch traced here: 242 us
  Pallas kernels  224 us (92%)
  other arithmetic  10.1 us (4%)
  local copies, waits for them, and re-layouts  7.27 us (3%)
    pallas_call x1, Pallas kernels, grads(): pl.pallas_call(grads_kernel, in_specs=[VM] * 6, out_specs=[VM] * 4, out_s...  70.2 us
    pallas_call x1, Pallas kernels, exchange(): pl.pallas_call(exchange_kernel, in_specs=[VM] * 4, out_specs=[VM] * 4, ou...  68.1 us
    pallas_call x1, Pallas kernels, book_sums(): pl.pallas_call(book_kernel, grid=(subs // 32,), in_specs=[pl.BlockSpec((3...  43.3 us
    pallas_call x1, Pallas kernels, score_grads(): pl.pallas_call(scores_kernel, in_specs=[VM] * 3, out_specs=[VM] * 2, out_...  26.1 us
    pallas_call x1, Pallas kernels, decode(): pl.pallas_call(decode_kernel, grid=(subs // step,), in_specs=[pl.BlockSpe...  15.9 us

profile of v2, /device:TPU:1, one launch (start us, length us, event | category | flops | bytes accessed | tf_op | source)
XLA Modules:
  0.0 241.9 jit_solution(9705444514231785601)
XLA Ops:
  0.6 0.0 copy-start
  0.6 0.0 copy-start.1
  0.7 0.9 fusion.5
  1.6 1.5 fusion
  3.1 0.8 dynamic-slice
  3.9 0.7 copy.15.column_ref
  4.6 0.0 copy-done
  4.6 0.7 dynamic-slice_bitcast_fusion.book_ref
  5.2 1.8 convert_bitcast_fusion.codes_ref
  7.0 0.0 copy-done.1
  7.0 0.2 convert_multiply_fusion.1
  7.3 0.7 fusion.2.slice_ref
  7.9 68.1 %exchange.1 = (bf16[8,128,256]{2,1,0:T(8,128)(2,1)}, bf16[256,2048]{1,0:T(8,128)(2,1)}, bf16[256,2048]{1,0:T(8,128)(2,1)}, bf16[8,256,256]{2,1,0:T(8,128)(2,1)}) custom-call(bf16[128,256]{1,0:T(8,128)(2,1)} %fusion.2.slice_ref, bf16[256,512]{1,0:T(8,128)(2,1)} %weight_ref.3, bf16[64,2048]{1,0:T(8,128)(2,1)} %convert_bitcast_fusion.codes_ref, ...), custom_call_target="tpu_custom_call" | custom-call | tf_op jit(solution)/shard_map/exchange/pallas_call | solution.py:380
  76.0 15.9 %decode.1.passages_ref = bf16[2048,2048]{1,0:T(8,128)(2,1)} custom-call(bf16[256,2048]{1,0:T(8,128)(2,1)} %get-tuple-element.15.codes_ref, bf16[2048,256]{1,0:T(8,128)(2,1)} %bitcast.19), custom_call_target="tpu_custom_call" | custom-call | tf_op jit(solution)/shard_map/decode/pallas_call | solution.py:34
  91.9 26.1 %score_grads.1 = (bf16[256,2048]{1,0:T(8,128)(2,1)}, f32[8,128]{1,0:T(8,128)}) custom-call(bf16[256,2048]{1,0:T(8,128)(2,1)} %get-tuple-element.14.queries_ref, bf16[2048,2048]{1,0:T(8,128)(2,1)} %decode.1.passages_ref, s32[128,1]{1,0:T(8,128)} %copy.15.column_ref), custom_call_target="tpu_custom_call" | custom-call | tf_op jit(solution)/shard_map/score_grads/pallas_call | solution.py:479
  118.1 43.3 %book_sums.1 = f32[32,64,256]{2,1,0:T(8,128)} custom-call(bf16[256,2048]{1,0:T(8,128)(2,1)} %get-tuple-element.15.codes_ref, bf16[256,2048]{1,0:T(8,128)(2,1)} %get-tuple-element.14.queries_ref, bf16[256,2048]{1,0:T(8,128)(2,1)} %get-tuple-element.17.sg_ref.grad_ref), custom_call_target="tpu_custom_call" | custom-call | tf_op jit(solution)/shard_map/book_sums/pallas_call | solution.py:69
  161.4 1.7 convert_element_type.29
  163.1 1.0 copy.20
  164.2 70.2 %grads.1 = (f32[256,512]{1,0:T(8,128)}, bf16[128,4096]{1,0:T(8,128)(2,1)}, f32[8,8,128]{2,1,0:T(8,128)}, bf16[2,4,64,256]{3,2,1,0:T(8,128)(2,1)}) custom-call(bf16[256,2048]{1,0:T(8,128)(2,1)} %get-tuple-element.17.sg_ref.grad_ref, bf16[2048,2048]{1,0:T(8,128)(2,1)} %decode.1.passages_ref, bf16[8,128,256]{2,1,0:T(8,128)(2,1)} %get-tuple-element.18.normed_ref, ...), custom_call_target="tpu_custom_call" | custom-call | tf_op jit(solution)/shard_map/grads/pallas_call | solution.py:655
  234.4 0.0 copy-start.2
  234.4 0.8 constant_dynamic-slice_fusion
  235.2 0.5 slice_bitcast_fusion
  235.7 0.0 copy-done.5
  235.7 1.6 fusion.1
  237.4 0.0 copy-done.2
  237.4 1.7 subtract_convert_fusion
  239.1 0.0 copy-done.4
  239.1 0.2 copy.17
  239.3 0.0 copy-start.3
  239.3 0.3 copy.18
  239.6 1.4 reshape.49
  241.1 0.8 copy.22
  (5 shorter events, 0.0 us)
Async XLA Ops:
  0.6 4.0 %copy-start = (bf16[64,8,256]{2,1,0:T(8,128)(2,1)S(1)}, bf16[64,8,256]{2,1,0:T(8,128)(2,1)}, u32[]{:S(2)}) copy-start(bf16[64,8,256]{2,1,0:T(8,128)(2,1)} %param.10) | copy-start | bytes 786436
  0.6 6.4 %copy-start.1 = (bf16[128,4096]{1,0:T(8,128)(2,1)S(1)}, bf16[128,4096]{1,0:T(8,128)(2,1)}, u32[]{:S(2)}) copy-start(bf16[128,4096]{1,0:T(8,128)(2,1)} %param.6) | copy-start | bytes 3145732
  164.2 71.5 %copy-start.5 = (f32[4096]{0:T(1024)S(1)}, f32[4096]{0:T(1024)}, u32[]{:S(2)}) copy-start(f32[4096]{0:T(1024)} %param.7) | copy-start | bytes 49156
  234.4 3.0 %copy-start.2 = (bf16[128,4096]{1,0:T(8,128)(2,1)S(1)}, bf16[128,4096]{1,0:T(8,128)(2,1)}, u32[]{:S(2)}) copy-start(bf16[128,4096]{1,0:T(8,128)(2,1)} %get-tuple-element.21) | copy-start | bytes 3145732
  237.3 1.7 copy-start.4
  239.3 1.8 copy-start.3

commit v3 on v2

--- a/solution.py
+++ b/solution.py
@@ -14,67 +14,92 @@
 norm_eps = 1e-06
 
 
-def decode_kernel(codes_ref, book_ref, out_ref):
-    subs, count = codes_ref.shape
-    for tile in range(count // 128):
-        block = codes_ref[:, tile * 128:(tile + 1) * 128].astype(jnp.float32).astype(jnp.int32)
-        found = []
-        for m in range(subs):
-            code = jnp.broadcast_to(block[m:m + 1, :], (8, 128))
-            low = code & 127
-            first = jnp.take_along_axis(book_ref[m * 8:m * 8 + 8, 0:128].astype(jnp.float32), low, axis=1, mode="promise_in_bounds")
-            second = jnp.take_along_axis(book_ref[m * 8:m * 8 + 8, 128:256].astype(jnp.float32), low, axis=1, mode="promise_in_bounds")
-            found.append(jnp.where(code >= 128, second, first))
-        for m in range(0, subs, 2):
-            out_ref[m * 8:m * 8 + 16, tile * 128:(tile + 1) * 128] = jnp.concatenate(found[m:m + 2], 0).astype(jnp.bfloat16)
-
-def decode(codes, book):
-    subs, count = codes.shape
-    step = 16
-    return pl.pallas_call(
-        decode_kernel,
-        grid=(subs // step,),
-        in_specs=[pl.BlockSpec((step, count), lambda i: (i, 0)), pl.BlockSpec((step * 8, 256), lambda i: (i, 0))],
-        out_specs=pl.BlockSpec((step * 8, count), lambda i: (i, 0)),
-        out_shape=jax.ShapeDtypeStruct((subs * 8, count), jnp.bfloat16),
-        name="decode",
-    )(codes, book)
-
-def book_kernel(codes_ref, queries_ref, sg_ref, out_ref, pg_ref, hot_ref, gw_ref):
-    count = codes_ref.shape[1]
-    pg_ref[...] = (lax.dot_general(queries_ref[...], sg_ref[...], (((0,), (0,)), ((), ())), preferred_element_type=jnp.float32) * 0.0625).astype(jnp.bfloat16)
-    levels = lax.broadcasted_iota(jnp.int32, (64, 128), 0)
-    for group in range(4):
-        for tile in range(count // 128):
-            at = slice(tile * 128, (tile + 1) * 128)
-            block = codes_ref[group * 8:group * 8 + 8, at].astype(jnp.float32).astype(jnp.int32)
-            for m in range(8):
-                row = block[m:m + 1, :]
-                hi = jnp.broadcast_to(row & 63, (64, 128))
-                hot_ref[m * 64:m * 64 + 64, at] = (hi == levels).astype(jnp.float32).astype(jnp.bfloat16)
-                lo = jnp.broadcast_to(row >> 6, (8, 128))
-                grad = pg_ref[group * 64 + m * 8:group * 64 + m * 8 + 8, at].astype(jnp.float32)
-                parts = [jnp.where(lo == t, grad, 0.0) for t in range(4)]
-                gw_ref[m * 32:m * 32 + 32, at] = jnp.concatenate(parts, 0).astype(jnp.bfloat16)
-        full = lax.dot_general(hot_ref[...], gw_ref[...], (((1,), (1,)), ((), ())), preferred_element_type=jnp.float32)
-        own = lax.broadcasted_iota(jnp.int32, (64, 256), 1) // 32
-        total = jnp.zeros((64, 256), jnp.float32)
-        for m in range(8):
-            total = jnp.where(own == m, full[m * 64:m * 64 + 64, :], total)
-        out_ref[group] = total
-
-def book_sums(codes, queries, sg):
-    subs, count = codes.shape
-    rows = queries.shape[0]
-    return pl.pallas_call(
-        book_kernel,
-        grid=(subs // 32,),
-        in_specs=[pl.BlockSpec((32, count), lambda i: (i, 0)), pl.BlockSpec((rows, 256), lambda i: (0, i)), pl.BlockSpec((rows, count), lambda i: (0, 0))],
-        out_specs=pl.BlockSpec((4, 64, 256), lambda i: (i, 0, 0)),
-        out_shape=jax.ShapeDtypeStruct((subs // 8, 64, 256), jnp.float32),
-        scratch_shapes=[pltpu.VMEM((256, count), jnp.bfloat16), pltpu.VMEM((512, count), jnp.bfloat16), pltpu.VMEM((256, count), jnp.bfloat16)],
-        name="book_sums",
-    )(codes, queries, sg)
+def decode_slice(g, codes_ref, book_ref, out_ref):
+    f32 = jnp.float32
+    block, part = lax.div(g, 2), lax.rem(g, 2)
+    rows = pl.ds(pl.multiple_of(g * 16, 16), 16)
+    books = []
+    for pair in range(8):
+        both_rows = book_ref[block, pl.ds(pl.multiple_of(part * 128 + pair * 16, 16), 16), :].astype(f32)
+        books += [both_rows[0:8], both_rows[8:16]]
+
+    def tile_step(tile, carry):
+        at = pl.ds(pl.multiple_of(tile * 128, 128), 128)
+        codes = codes_ref[rows, at].astype(f32).astype(jnp.int32)
+        for pair in range(8):
+            found = []
+            for m in (pair * 2, pair * 2 + 1):
+                code = jnp.broadcast_to(codes[m : m + 1, :], (8, 128))
+                low = code & 127
+                picked = [
+                    jnp.take_along_axis(
+                        books[m][:, half * 128 : half * 128 + 128], low, axis=1,
+                        mode="promise_in_bounds",
+                    )
+                    for half in range(2)
+                ]
+                found.append(jnp.where(code >= 128, picked[1], picked[0]))
+            out_ref[pl.ds(pl.multiple_of(g * 128 + pair * 16, 16), 16), at] = jnp.concatenate(
+                found, 0
+            ).astype(jnp.bfloat16)
+        return carry
+
+    lax.fori_loop(0, codes_ref.shape[1] // 128, tile_step, 0, unroll=16)
+
+
+def split_codes(codes_ref, hi_ref, lo_ref):
+    whole = codes_ref[...].astype(jnp.float32)
+    lo = jnp.floor(whole * (1.0 / 64.0))
+    lo_ref[...] = lo
+    hi_ref[...] = whole - lo * 64.0
+
+def book_block(b, hi_ref, lo_ref, queries_ref, grad_ref, pg_ref, hot_ref, gw_ref, put):
+    b16, f32 = jnp.bfloat16, jnp.float32
+    count = grad_ref.shape[1]
+    pg_ref[...] = (
+        lax.dot_general(
+            queries_ref[:, pl.ds(pl.multiple_of(b * 256, 256), 256)], grad_ref[...],
+            (((0,), (0,)), ((), ())), preferred_element_type=f32,
+        ) * score_scale
+    ).astype(b16)
+    sublane = lax.broadcasted_iota(jnp.int32, (16, 128), 0).astype(f32)
+    levels = [(sublane + 16.0 * j).astype(b16) for j in range(4)]
+    upper = lax.broadcasted_iota(jnp.int32, (16, 128), 0) >= 8
+    picks = [jnp.where(upper, 2.0 * j + 1.0, 2.0 * j).astype(b16) for j in range(2)]
+    one, zero = jnp.ones((16, 128), b16), jnp.zeros((16, 128), b16)
+    own = lax.div(lax.broadcasted_iota(jnp.int32, (64, 256), 1), 32)
+
+    def group_step(group, carry):
+        rows = pl.ds(pl.multiple_of(b * 32 + group * 8, 8), 8)
+
+        def tile_step(tile, carry):
+            at = pl.ds(pl.multiple_of(tile * 128, 128), 128)
+            hi_block, lo_block = hi_ref[rows, at], lo_ref[rows, at]
+            for pair in range(4):
+                grads = pg_ref[pl.ds(pl.multiple_of(group * 64 + pair * 16, 16), 16), at].astype(f32)
+                for side in range(2):
+                    m = pair * 2 + side
+                    hi = jnp.broadcast_to(hi_block[m : m + 1, :], (16, 128)).astype(b16)
+                    lo = jnp.broadcast_to(lo_block[m : m + 1, :], (16, 128)).astype(b16)
+                    for j in range(4):
+                        hot_ref[m * 64 + j * 16 : m * 64 + j * 16 + 16, at] = jnp.where(hi == levels[j], one, zero)
+                    one_grad = grads[side * 8 : side * 8 + 8]
+                    twice = jnp.concatenate([one_grad, one_grad], 0).astype(b16)
+                    for j in range(2):
+                        gw_ref[m * 32 + j * 16 : m * 32 + j * 16 + 16, at] = jnp.where(lo == picks[j], twice, zero)
+            return carry
+
+        lax.fori_loop(0, count // 128, tile_step, 0, unroll=16)
+        full = lax.dot_general(
+            hot_ref[...], gw_ref[...], (((1,), (1,)), ((), ())), preferred_element_type=f32
+        )
+        total = full[0:64]
+        for m in range(1, 8):
+            total = jnp.where(own == m, full[m * 64 : m * 64 + 64], total)
+        put(group, b, total.astype(b16))
+        return carry
+
+    lax.fori_loop(0, 4, group_step, 0)
 
 
 def ring(c, step):
@@ -183,12 +208,6 @@
         end()
 
 
-def run_together(*parts):
-    live = list(parts)
-    while live:
-        live = [p for p in live if next(p, live) is not live]
-
-
 def both(*parts):
     live = list(parts)
     while live:
@@ -236,10 +255,17 @@
     return ref.at[rows * side : rows * side + rows]
 
 
+def in_turns(order, **parts):
+    live = set(parts)
+    for name in list(order) + sorted(parts) * 64:
+        if name in live and next(parts[name], live) is live:
+            live.remove(name)
+
+
 def exchange_kernel(
     slice_ref, weight_ref, codes_ref, book_ref,
-    normed_ref, queries_ref, codes_all_ref, book_all_ref,
-    other_ref, came_ref, acc_ref, up_ref, down_ref, from_up_ref, from_down_ref, far_ref, piece_ref,
+    normed_ref, queries_ref, codes_all_ref, passages_ref,
+    book_all_ref, other_ref, came_ref, acc_ref, up_ref, down_ref, from_up_ref, from_down_ref, far_ref, piece_ref,
     send_sems, recv_sems,
 ):
     at = Place()
@@ -251,125 +277,149 @@
         + [at.core(), at.along_y(1), at.along_y(-1), at.far_x()]
         + [{"xh": 1 - at.xh, "xl": 1 - at.xl}]
     )
-    sent = []
-    mine = pl.ds(pl.multiple_of(at.y * 512 + at.k * 256, 256), 256)
-    rows_here = pl.ds(pl.multiple_of(at.qry * 32, 32), 32)
-    for cross in range(2):
-        k = at.k if cross == 0 else 1 - at.k
-        rows_there = pl.ds(pl.multiple_of(k * 32, 32), 32)
-        for peer in ([] if cross == 0 else [{}]) + group:
-            q = peer["z"] * 2 + peer["xl"] if peer else at.qry
-            sent.append(
-                wires.send(
-                    codes_ref.at[rows_there, pl.ds(pl.multiple_of(q * 256, 256), 256)],
-                    codes_all_ref.at[rows_here, mine],
-                    {"k": k, **peer},
-                )
-            )
-    codes_all_ref[rows_here, mine] = codes_ref[
-        pl.ds(pl.multiple_of(at.k * 32, 32), 32),
-        pl.ds(pl.multiple_of(at.qry * 256, 256), 256),
-    ]
 
     def column(ref, flip):
         return lambda s: ref.at[ring(at.z, s) * 2 + (at.xl if flip == 0 else 1 - at.xl)]
 
-    partner = {"xl": 1 - at.xl}
-    gathers = []
-    for own, out in ((slice_ref, normed_ref), (book_ref, book_all_ref)):
-        side = wires.send(own, out.at[at.qry], partner)
-        gathers.append((side, out, ring_gather(wires, at.along_z, own, column(out, 0), rows_half)))
-    normed_ref[at.qry] = slice_ref[...]
-    book_all_ref[at.qry] = book_ref[...]
-    ends = []
-    for side, out, forward in gathers:
+    def group_gather(own, out):
+        near, far = column(out, 0), column(out, 1)
+        side = wires.send(own, out.at[at.qry], {"xl": 1 - at.xl})
+        forward = ring_gather(wires, at.along_z, own, near, rows_half)
+        out[at.qry] = own[...]
+        yield
         side.wait_recv()
-        far = column(out, 1)
-        second = ring_gather(wires, at.along_z, far(0), far, rows_half)
-        ends.append((forward(), second))
-    normed_end = ends[0][1]()
-    ends[0][0]()
-    normed_end()
-
-    order = (2, 1, -1, 0)
-    crossed = []
-    for s in order:
-        b = ring(at.y, s)
-        left = normed_ref[pl.ds(b * 2, 2)].reshape(256, 256)
-        other_ref[b] = jnp.dot(
-            left,
-            weight_ref[:, pl.ds(pl.multiple_of((1 - at.k) * 256, 256), 256)],
-            preferred_element_type=jnp.float32,
+        forward_far = ring_gather(wires, at.along_z, far(0), far, rows_half)
+        yield
+        finish = forward()
+        yield
+        finish_far = forward_far()
+        yield
+        finish()
+        finish_far()
+
+    def main():
+        yield from group_gather(slice_ref, normed_ref)
+        order = (2, 1, -1, 0)
+        crossed = []
+        for s in order:
+            b = ring(at.y, s)
+            left = normed_ref[pl.ds(b * 2, 2)].reshape(256, 256)
+            other_ref[b] = jnp.dot(
+                left,
+                weight_ref[:, pl.ds(pl.multiple_of((1 - at.k) * 256, 256), 256)],
+                preferred_element_type=jnp.float32,
+            )
+            crossed.append(wires.send(other_ref.at[b], came_ref.at[b], at.core()))
+        for s in order:
+            b = ring(at.y, s)
+            left = normed_ref[pl.ds(b * 2, 2)].reshape(256, 256)
+            acc_ref[b] = jnp.dot(
+                left,
+                weight_ref[:, pl.ds(pl.multiple_of(at.k * 256, 256), 256)],
+                preferred_element_type=jnp.float32,
+            )
+        far_y, next_y, last_y = ring(at.y, 2), ring(at.y, 1), ring(at.y, -1)
+        crossed[0].wait_recv()
+        acc_ref[far_y] = acc_ref[far_y] + came_ref[far_y]
+        up = wires.send(acc_ref.at[far_y, 0:128], up_ref, at.along_y(1))
+        down = wires.send(acc_ref.at[far_y, 128:256], down_ref, at.along_y(-1))
+        crossed[1].wait_recv()
+        acc_ref[next_y] = acc_ref[next_y] + came_ref[next_y]
+        crossed[2].wait_recv()
+        acc_ref[last_y] = acc_ref[last_y] + came_ref[last_y]
+        crossed[3].wait_recv()
+        acc_ref[at.y] = acc_ref[at.y] + came_ref[at.y]
+        yield
+        up.wait_recv()
+        acc_ref[next_y, 0:128] = acc_ref[next_y, 0:128] + up_ref[...]
+        up = wires.send(acc_ref.at[next_y], from_up_ref, at.along_y(1))
+        down.wait_recv()
+        acc_ref[last_y, 128:256] = acc_ref[last_y, 128:256] + down_ref[...]
+        down = wires.send(acc_ref.at[last_y], from_down_ref, at.along_y(-1))
+        yield
+        up.wait_recv()
+        down.wait_recv()
+        acc_ref[at.y] = acc_ref[at.y] + from_up_ref[...] + from_down_ref[...]
+        far_rows = pl.ds(pl.multiple_of((1 - at.xh) * 128, 128), 128)
+        own_rows = pl.ds(pl.multiple_of(at.xh * 128, 128), 128)
+        across = wires.send(acc_ref.at[at.y, far_rows], far_ref, at.far_x())
+        yield
+        across.wait_recv()
+        piece_ref[...] = (acc_ref[at.y, own_rows] + far_ref[...]).astype(jnp.bfloat16)
+
+        def spot(x, z):
+            q = z * 2 + lax.rem(x, 2)
+            row = pl.multiple_of(lax.div(x, 2) * 128, 128)
+            return row, pl.ds(pl.multiple_of(q * 256, 256), 256)
+
+        def colour(n, x, z):
+            row, cols = spot(x, z)
+            return queries_ref.at[pl.ds(row + n * 64, 64), cols]
+
+        row, cols = spot(at.x, at.z)
+        queries_ref[pl.ds(row, 128), cols] = piece_ref[...]
+        yield from both(
+            torus_gather(
+                wires, at.along_x, at.along_z, piece_ref.at[0:64],
+                lambda i, j: colour(0, ring(at.x, i), ring(at.z, j)), rows_half,
+            ),
+            torus_gather(
+                wires, at.along_z, at.along_x, piece_ref.at[64:128],
+                lambda i, j: colour(1, ring(at.x, j), ring(at.z, i)), rows_half,
+            ),
         )
-        crossed.append(wires.send(other_ref.at[b], came_ref.at[b], at.core()))
-    for s in order:
-        b = ring(at.y, s)
-        left = normed_ref[pl.ds(b * 2, 2)].reshape(256, 256)
-        acc_ref[b] = jnp.dot(
-            left,
-            weight_ref[:, pl.ds(pl.multiple_of(at.k * 256, 256), 256)],
-            preferred_element_type=jnp.float32,
-        )
-    far_y, next_y, last_y = ring(at.y, 2), ring(at.y, 1), ring(at.y, -1)
-    crossed[0].wait_recv()
-    acc_ref[far_y] = acc_ref[far_y] + came_ref[far_y]
-    up = wires.send(acc_ref.at[far_y, 0:128], up_ref, at.along_y(1))
-    down = wires.send(acc_ref.at[far_y, 128:256], down_ref, at.along_y(-1))
-    crossed[1].wait_recv()
-    acc_ref[next_y] = acc_ref[next_y] + came_ref[next_y]
-    crossed[2].wait_recv()
-    acc_ref[last_y] = acc_ref[last_y] + came_ref[last_y]
-    crossed[3].wait_recv()
-    acc_ref[at.y] = acc_ref[at.y] + came_ref[at.y]
-    up.wait_recv()
-    acc_ref[next_y, 0:128] = acc_ref[next_y, 0:128] + up_ref[...]
-    up = wires.send(acc_ref.at[next_y], from_up_ref, at.along_y(1))
-    down.wait_recv()
-    acc_ref[last_y, 128:256] = acc_ref[last_y, 128:256] + down_ref[...]
-    down = wires.send(acc_ref.at[last_y], from_down_ref, at.along_y(-1))
-
-    for copy in sent:
-        copy.wait_recv()
-
-    def chunk(s):
-        return codes_all_ref.at[:, pl.ds(pl.multiple_of(ring(at.y, s) * 512, 512), 512)]
-
-    codes_forward = ring_gather(wires, at.along_y, chunk(0), chunk, rows_half)
-
-    up.wait_recv()
-    down.wait_recv()
-    acc_ref[at.y] = acc_ref[at.y] + from_up_ref[...] + from_down_ref[...]
-    far_rows = pl.ds(pl.multiple_of((1 - at.xh) * 128, 128), 128)
-    own_rows = pl.ds(pl.multiple_of(at.xh * 128, 128), 128)
-    across = wires.send(acc_ref.at[at.y, far_rows], far_ref, at.far_x())
-    across.wait_recv()
-    piece_ref[...] = (acc_ref[at.y, own_rows] + far_ref[...]).astype(jnp.bfloat16)
-
-    def spot(x, z):
-        q = z * 2 + lax.rem(x, 2)
-        return pl.multiple_of(lax.div(x, 2) * 128, 128), pl.ds(pl.multiple_of(q * 256, 256), 256)
-
-    def colour(n, x, z):
-        row, cols = spot(x, z)
-        return queries_ref.at[pl.ds(row + n * 64, 64), cols]
-
-    row, cols = spot(at.x, at.z)
-    queries_ref[pl.ds(row, 128), cols] = piece_ref[...]
-    run_together(
-        torus_gather(
-            wires, at.along_x, at.along_z, piece_ref.at[0:64],
-            lambda i, j: colour(0, ring(at.x, i), ring(at.z, j)), rows_half,
-        ),
-        torus_gather(
-            wires, at.along_z, at.along_x, piece_ref.at[64:128],
-            lambda i, j: colour(1, ring(at.x, j), ring(at.z, i)), rows_half,
-        ),
+
+    def codes_chain():
+        sent = []
+        mine = pl.ds(pl.multiple_of(at.y * 512 + at.k * 256, 256), 256)
+        rows_here = pl.ds(pl.multiple_of(at.qry * 32, 32), 32)
+        for cross in range(2):
+            k = at.k if cross == 0 else 1 - at.k
+            rows_there = pl.ds(pl.multiple_of(k * 32, 32), 32)
+            for peer in ([] if cross == 0 else [{}]) + group:
+                q = peer["z"] * 2 + peer["xl"] if peer else at.qry
+                sent.append(
+                    wires.send(
+                        codes_ref.at[rows_there, pl.ds(pl.multiple_of(q * 256, 256), 256)],
+                        codes_all_ref.at[rows_here, mine],
+                        {"k": k, **peer},
+                    )
+                )
+        codes_all_ref[rows_here, mine] = codes_ref[
+            pl.ds(pl.multiple_of(at.k * 32, 32), 32),
+            pl.ds(pl.multiple_of(at.qry * 256, 256), 256),
+        ]
+        yield
+        for copy in sent:
+            copy.wait_recv()
+
+        def chunk(s):
+            return codes_all_ref.at[:, pl.ds(pl.multiple_of(ring(at.y, s) * 512, 512), 512)]
+
+        forward = ring_gather(wires, at.along_y, chunk(0), chunk, rows_half)
+        yield
+        finish = forward()
+        yield
+        finish()
+
+    def decoded():
+        for g in range(0, 16, 2):
+
+            def step(n, carry):
+                decode_slice(n, codes_all_ref, book_all_ref, passages_ref)
+                return carry
+
+            lax.fori_loop(g, g + 2, step, 0)
+            yield
+
+    in_turns(
+        EXCHANGE_ORDER,
+        m=main(), c=codes_chain(), b=group_gather(book_ref, book_all_ref), d=decoded(),
     )
-    book_end = ends[1][1]()
-    ends[1][0]()
-    book_end()
-    codes_forward()()
     wires.drain()
+
+
+EXCHANGE_ORDER = "mc" + "m" + "m" + "c" + "m" + "b" + "m" + "b" + "c" + "bb" + "m" + "bc" + "d" + "m" + "d" + "m" + "dmdmdmdmdmdm"
 
 
 VM = pl.BlockSpec(memory_space=pltpu.VMEM)
@@ -385,9 +435,10 @@
             jax.ShapeDtypeStruct((8, 128, 256), b16),
             jax.ShapeDtypeStruct((256, 2048), b16),
             jax.ShapeDtypeStruct((256, 2048), b16),
-            jax.ShapeDtypeStruct((8, 256, 256), b16),
+            jax.ShapeDtypeStruct((2048, 2048), b16),
         ],
         scratch_shapes=[
+            pltpu.VMEM((8, 256, 256), b16),
             pltpu.VMEM((4, 256, 256), f32),
             pltpu.VMEM((4, 256, 256), f32),
             pltpu.VMEM((4, 256, 256), f32),
@@ -525,10 +576,10 @@
 
 
 def grads_kernel(
-    grad_ref, passages_ref, normed_ref, weight_ref, losses_ref, sums_ref,
+    grad_ref, passages_ref, normed_ref, weight_ref, losses_ref, codes_ref, queries_ref,
     weight_grad_ref, norm_ref, losses_all_ref, book_ref,
     part_ref, x_half, x_full, z_half, z_full, piece_ref, query_ref, term_ref, terms_ref, norm_piece_ref,
-    add_ref, y_half, y_full, share_ref, far_ref, final_ref,
+    add_ref, y_half, y_full, share_ref, far_ref, final_ref, hi_ref, lo_ref, pg_ref, hot_ref, gw_ref,
     send_sems, recv_sems,
 ):
     at = Place()
@@ -541,7 +592,15 @@
     losses_all_ref[places] = losses_ref[...]
 
     def book_sums_over_devices():
-        add_ref[...] = sums_ref[...]
+        def put(group, b, sums):
+            add_ref[group, b] = sums
+
+        split_codes(codes_ref, hi_ref, lo_ref)
+        for b in range(8):
+            book_block(
+                b, hi_ref, lo_ref, queries_ref, grad_ref, pg_ref, hot_ref, gw_ref, put
+            )
+            yield
         yield from ring_sum(
             wires, at.along_y, lambda s: add_ref.at[ring(at.y, s)], middle_half,
             (y_half.at[0], y_half.at[1], y_full.at[0], y_full.at[1]),
@@ -644,17 +703,20 @@
         column(at.xh, at.y, at.k)[...] = norm_piece_ref[...]
         yield from psg_gather(wires, at, norm_piece_ref, column)
 
-    run_together(main(), book_sums_over_devices())
+    in_turns(GRADS_ORDER, m=main(), b=book_sums_over_devices())
     for copy in lost:
         copy.wait_recv()
     wires.drain()
 
 
-def grads(all_grad, passages, normed, weight, losses, sums):
+GRADS_ORDER = "mb" + "mbb" + "mb" + "mb" + "mb" + "mb" + "mb" + "bmbmbmbmbmbmbmbmb"
+
+
+def grads(all_grad, passages, normed, weight, losses, codes, queries):
     f32, b16 = jnp.float32, jnp.bfloat16
     return pl.pallas_call(
         grads_kernel,
-        in_specs=[VM] * 6,
+        in_specs=[VM] * 7,
         out_specs=[VM] * 4,
         out_shape=[
             jax.ShapeDtypeStruct((256, 512), f32),
@@ -679,12 +741,17 @@
             pltpu.VMEM((7, 64, 256), b16),
             pltpu.VMEM((64, 256), b16),
             pltpu.VMEM((2, 64, 256), b16),
+            pltpu.VMEM((256, 2048), f32),
+            pltpu.VMEM((256, 2048), f32),
+            pltpu.VMEM((256, 2048), b16),
+            pltpu.VMEM((512, 2048), b16),
+            pltpu.VMEM((256, 2048), b16),
             pltpu.SemaphoreType.DMA((112,)),
             pltpu.SemaphoreType.DMA((112,)),
         ],
         compiler_params=pltpu.CompilerParams(collective_id=2, has_side_effects=True),
         name="grads",
-    )(all_grad, passages, normed, weight, losses, sums)
+    )(all_grad, passages, normed, weight, losses, codes, queries)
 
 
 def unfold(sums):
@@ -710,8 +777,7 @@
     slice_own = lax.dynamic_slice_in_dim(normed_own, psg * row_span, row_span, 1)
     codes = pq_codes.T.astype(jnp.bfloat16)
     book_half = lax.dynamic_slice_in_dim(codebook, k * half, half, 0).reshape(half * 8, 256)
-    normed, queries, codes, book = exchange(slice_own, proj_weight, codes, book_half)
-    passages = decode(codes, book.reshape(2048, 256))
+    normed, queries, codes, passages = exchange(slice_own, proj_weight, codes, book_half)
 
     block = y * 2 + k
     targets = lax.dynamic_slice_in_dim(positives, block * own_rows, own_rows, 0)
@@ -721,10 +787,8 @@
     here = (shard // 8 == xh) & (sixth == qry)
     column = jnp.where(here, (shard % 8) * piece + inside % piece, -1)
     all_grad, block_losses = score_grads(queries, passages, column[:, None])
-    sums = book_sums(codes, queries, all_grad).astype(jnp.bfloat16)
-    sums = sums.reshape(8, 4, 64, 256).transpose(1, 0, 2, 3)
     weight_grad, norm_back, all_losses, book_grad = grads(
-        all_grad, passages, normed, proj_weight, block_losses, sums
+        all_grad, passages, normed, proj_weight, block_losses, codes, queries
     )
     losses = lax.dynamic_index_in_dim(all_losses, qry, 0, keepdims=False)[0]
     codebook_grad = unfold(book_grad.reshape(8, 64, 256).astype(jnp.float32))

time: 243 us -> 188 us (0.77)
  Pallas kernels: 224 us -> 172 us
    pallas_call x3 -> x1, Pallas kernels: 129 us -> 84.7 us  [grads(): pl.pallas_call(grads_kernel, in_specs=[VM] * 7, out_specs=[VM] * 4, out_s...]
    pallas_call x1, Pallas kernels: 26.1 us -> 22.6 us  [score_grads(): pl.pallas_call(scores_kernel, in_specs=[VM] * 3, out_specs=[VM] * 2, out_...]
    pallas_call x1, Pallas kernels: 68.1 us -> 64.9 us  [exchange(): pl.pallas_call(exchange_kernel, in_specs=[VM] * 4, out_specs=[VM] * 4, ou...]
where the time goes in v3:
time: 188 us
  Pallas kernels  172 us (91%)
  other arithmetic  8.41 us (4%)
  local copies, waits for them, and re-layouts  6.16 us (3%)
    pallas_call x1, Pallas kernels, grads(): pl.pallas_call(grads_kernel, in_specs=[VM] * 7, out_specs=[VM] * 4, out_s...  84.7 us
    pallas_call x1, Pallas kernels, exchange(): pl.pallas_call(exchange_kernel, in_specs=[VM] * 4, out_specs=[VM] * 4, ou...  64.9 us
    pallas_call x1, Pallas kernels, score_grads(): pl.pallas_call(scores_kernel, in_specs=[VM] * 3, out_specs=[VM] * 2, out_...  22.6 us

profile of v3, /device:TPU:1, one launch (start us, length us, event | category | flops | bytes accessed | tf_op | source)
XLA Modules:
  0.0 187.6 jit_solution(11399666003111400498)
XLA Ops:
  0.6 0.0 copy-start
  0.6 0.0 copy-start.1
  0.7 0.9 fusion.5
  1.6 1.5 fusion
  3.1 0.8 dynamic-slice
  3.9 0.7 copy.14.column_ref
  4.6 0.0 copy-done
  4.6 0.7 dynamic-slice_bitcast_fusion.book_ref
  5.2 1.8 convert_bitcast_fusion.codes_ref
  7.0 0.0 copy-done.1
  7.0 0.2 convert_multiply_fusion.1
  7.3 0.7 fusion.2.slice_ref
  7.9 64.9 %exchange.1 = (bf16[8,128,256]{2,1,0:T(8,128)(2,1)}, bf16[256,2048]{1,0:T(8,128)(2,1)}, bf16[256,2048]{1,0:T(8,128)(2,1)}, bf16[2048,2048]{1,0:T(8,128)(2,1)}) custom-call(bf16[128,256]{1,0:T(8,128)(2,1)} %fusion.2.slice_ref, bf16[256,512]{1,0:T(8,128)(2,1)} %weight_ref.3, bf16[64,2048]{1,0:T(8,128)(2,1)} %convert_bitcast_fusion.codes_ref, ...), custom_call_target="tpu_custom_call" | custom-call | tf_op jit(solution)/shard_map/exchange/pallas_call | solution.py:430
  72.9 22.6 %score_grads.1 = (bf16[256,2048]{1,0:T(8,128)(2,1)}, f32[8,128]{1,0:T(8,128)}) custom-call(bf16[256,2048]{1,0:T(8,128)(2,1)} %get-tuple-element.14.queries_ref, bf16[2048,2048]{1,0:T(8,128)(2,1)} %get-tuple-element.15.passages_ref, s32[128,1]{1,0:T(8,128)} %copy.14.column_ref), custom_call_target="tpu_custom_call" | custom-call | tf_op jit(solution)/shard_map/score_grads/pallas_call | solution.py:530
  95.5 0.0 copy-start.5
  95.5 84.7 %grads.1 = (f32[256,512]{1,0:T(8,128)}, bf16[128,4096]{1,0:T(8,128)(2,1)}, f32[8,8,128]{2,1,0:T(8,128)}, bf16[2,4,64,256]{3,2,1,0:T(8,128)(2,1)}) custom-call(bf16[256,2048]{1,0:T(8,128)(2,1)} %get-tuple-element.16.grad_ref, bf16[2048,2048]{1,0:T(8,128)(2,1)} %get-tuple-element.15.passages_ref, bf16[8,128,256]{2,1,0:T(8,128)(2,1)} %get-tuple-element.17.normed_ref, ...), custom_call_target="tpu_custom_call" | custom-call | tf_op jit(solution)/shard_map/grads/pallas_call | solution.py:717
  180.2 0.0 copy-start.2
  180.2 0.8 constant_dynamic-slice_fusion
  181.0 0.5 slice_bitcast_fusion
  181.5 0.0 copy-done.5
  181.5 1.6 fusion.1
  183.2 0.0 copy-start.4
  183.2 0.0 copy-done.2
  183.2 1.7 subtract_convert_fusion
  184.9 0.0 copy-done.4
  184.9 0.2 copy.15
  185.1 0.0 copy-start.3
  185.1 0.3 copy.16
  185.4 1.4 reshape.41
  186.8 0.0 copy-done.3
  186.8 0.8 copy.18
  (2 shorter events, 0.0 us)
Async XLA Ops:
  0.6 4.0 %copy-start = (bf16[64,8,256]{2,1,0:T(8,128)(2,1)S(1)}, bf16[64,8,256]{2,1,0:T(8,128)(2,1)}, u32[]{:S(2)}) copy-start(bf16[64,8,256]{2,1,0:T(8,128)(2,1)} %param.10) | copy-start | bytes 786436
  0.6 6.4 %copy-start.1 = (bf16[128,4096]{1,0:T(8,128)(2,1)S(1)}, bf16[128,4096]{1,0:T(8,128)(2,1)}, u32[]{:S(2)}) copy-start(bf16[128,4096]{1,0:T(8,128)(2,1)} %param.6) | copy-start | bytes 3145732
  95.5 86.0 %copy-start.5 = (f32[4096]{0:T(1024)S(1)}, f32[4096]{0:T(1024)}, u32[]{:S(2)}) copy-start(f32[4096]{0:T(1024)} %param.7) | copy-start | bytes 49156
  180.2 3.0 %copy-start.2 = (bf16[128,4096]{1,0:T(8,128)(2,1)S(1)}, bf16[128,4096]{1,0:T(8,128)(2,1)}, u32[]{:S(2)}) copy-start(bf16[128,4096]{1,0:T(8,128)(2,1)} %get-tuple-element.21) | copy-start | bytes 3145732
  183.2 1.7 copy-start.4
  185.1 1.7 copy-start.3
